TPU v7x, 128 devices: a whole 4x4x4 slice. The times are simulated.
128 devices in a mesh: gx: 32 (over x, y, core), gy: 4 (over z).
Axes of the slice: x: 4, y: 4, z: 4, core: 2. Of those that a mesh axis runs over, the one named last changes fastest.
Arguments:
- candidate_owner: int32 [1024, 512, 1], P(('gx', 'gy')), may hold values from 0 to 127; in each aligned block of 4096 rows (0 to 4095, 4096 to 8191, ..., all dimensions but the last counted through in order) at most 64 rows name the same one
- candidate_row: int32 [1024, 512], P(('gx', 'gy')), may hold values from 0 to 78335
- item_table: bfloat16 [10027008, 128], P(('gx', 'gy')), may hold values from -6 to 6
- w_in: bfloat16 [128, 512], replicated, may hold values from -0.5 to 0.5
- w_qkv: bfloat16 [1, 512, 1536], replicated, may hold values from -0.25 to 0.25
- w_out: bfloat16 [1, 512, 512], replicated, may hold values from -0.25 to 0.25
- w_up: bfloat16 [1, 512, 1024], replicated, may hold values from -0.25 to 0.25
- w_down: bfloat16 [1, 1024, 512], replicated, may hold values from -0.1875 to 0.1875
- norm_gains: float32 [1, 2, 512], replicated, may hold values from 0.25 to 1.75
- final_gain: float32 [512], replicated, may hold values from 0.25 to 1.75
- w_score: bfloat16 [512], replicated, may hold values from -0.25 to 0.25
Outputs:
- log_probs: float32 [1024, 512], P(('gx', 'gy'))
Inputs may be any that keep to these rules, and one draw needn't show every extreme that they name: `candidate_owner`: among the candidates of one device's 8 slates no shard is named more than 64 times, a bound that some block reaches.
All inputs are finite; a program needn't handle non-finite values.
Results may differ from a plain program's by a relative error of at most 0.0007.
Values may be sent and summed in bfloat16 or wider, within the bound.
A program may use at most 128 MiB of HBM per device.

v0:
```python
import jax
import jax.numpy as jnp
from jax import lax
from jax.sharding import PartitionSpec as P

HEADS = 8


def in_blocks(value, dim, count):
    lengths = value.shape
    parts = value.reshape(*lengths[:dim], count, lengths[dim] // count, *lengths[dim + 1 :])
    return jnp.moveaxis(parts, dim, 0)


def in_order(parts, dim):
    parts = jnp.moveaxis(parts, 0, dim)
    lengths = parts.shape
    return parts.reshape(*lengths[:dim], lengths[dim] * lengths[dim + 1], *lengths[dim + 2 :])


def joined_exchange(value, axis, axes, splits, concats):
    sizes = [lax.axis_size(a) for a in axes]
    parts = in_blocks(value, splits[0], sizes[0])
    parts = jnp.moveaxis(in_blocks(parts, splits[1] + 1, sizes[1]), 0, 1)
    inside = parts.shape[2:]
    parts = parts.reshape(-1, *inside)
    parts = lax.all_to_all(parts, axis, split_axis=0, concat_axis=0, tiled=True)
    parts = in_order(parts.reshape(*sizes, *inside), concats[0] + 1)
    return in_order(parts, concats[1])


def layer_norm(values, gain):
    mean = jnp.mean(values, axis=-1, keepdims=True)
    centred = values - mean
    variance = jnp.mean(centred * centred, axis=-1, keepdims=True)
    return centred * lax.rsqrt(variance + 1e-05) * gain


def attend_slate(operands):
    query, keys, values = operands
    length = query.shape[0]
    head_dim = query.shape[-1]
    scores = jnp.einsum(
        "qhd,khd->hqk", query, keys, preferred_element_type=jnp.float32
    ) * head_dim ** (-0.5)
    probs = jax.nn.softmax(scores, axis=-1).astype(jnp.bfloat16)
    mixed = jnp.einsum("hqk,khd->qhd", probs, values, preferred_element_type=jnp.float32)
    return mixed.astype(jnp.bfloat16).reshape(length, HEADS * head_dim)


def score_slates(emb, w_in, w_qkv, w_out, w_up, w_down, norm_gains, final_gain, w_score):
    slates, length, width = emb.shape
    model = w_in.shape[1]
    head_dim = model // HEADS
    resid = jnp.dot(emb.reshape(slates * length, width), w_in, preferred_element_type=jnp.float32)
    normed = layer_norm(resid, norm_gains[0, 0]).astype(jnp.bfloat16)
    weights = w_qkv[0]
    query = jnp.dot(normed, weights[:, :model], preferred_element_type=jnp.float32).astype(
        jnp.bfloat16
    )
    keys = jnp.dot(
        normed, weights[:, model : 2 * model], preferred_element_type=jnp.float32
    ).astype(jnp.bfloat16)
    values = jnp.dot(normed, weights[:, 2 * model :], preferred_element_type=jnp.float32).astype(
        jnp.bfloat16
    )
    query = query.reshape(slates, length, HEADS, head_dim)
    keys = keys.reshape(slates, length, HEADS, head_dim)
    values = values.reshape(slates, length, HEADS, head_dim)
    mixed = lax.map(attend_slate, (query, keys, values)).reshape(slates * length, model)
    resid = resid + jnp.dot(mixed, w_out[0], preferred_element_type=jnp.float32)
    normed = layer_norm(resid, norm_gains[0, 1]).astype(jnp.bfloat16)
    inner = jax.nn.gelu(jnp.dot(normed, w_up[0], preferred_element_type=jnp.float32)).astype(
        jnp.bfloat16
    )
    resid = resid + jnp.dot(inner, w_down[0], preferred_element_type=jnp.float32)
    final = layer_norm(resid, final_gain)
    logits = jnp.sum(final * w_score.astype(jnp.float32)[None, :], axis=-1)
    return jax.nn.log_softmax(logits.reshape(slates, length), axis=-1)


def slot_numbers(owner, shards, length):
    total = owner.shape[0]
    onehot = (owner[:, None] == jnp.arange(shards, dtype=jnp.int32)[None, :]).astype(jnp.bfloat16)
    blocks = onehot.reshape(total // length, length, shards)
    lower = (jnp.arange(length)[:, None] >= jnp.arange(length)[None, :]).astype(jnp.bfloat16)
    within = jnp.einsum("ij,bjn->bin", lower, blocks, preferred_element_type=jnp.float32)
    totals = within[:, -1, :]
    before = jnp.cumsum(totals, axis=0) - totals
    counts = within + before[:, None, :]
    picked = jnp.sum(counts * blocks.astype(jnp.float32), axis=-1)
    return (picked.reshape(total) - 1.0).astype(jnp.int32)


def fetch_rows(item_table, wanted):
    flat = wanted.reshape(-1)
    rows = jnp.take(item_table, jnp.maximum(flat, 0), axis=0)
    rows = jnp.where((flat >= 0)[:, None], rows, jnp.zeros_like(rows))
    return rows.reshape(wanted.shape + (item_table.shape[1],))


def per_device(
    candidate_owner,
    candidate_row,
    item_table,
    w_in,
    w_qkv,
    w_out,
    w_up,
    w_down,
    norm_gains,
    final_gain,
    w_score,
):
    slates, length, unused = candidate_owner.shape
    width = item_table.shape[1]
    shards = lax.axis_size(("gx", "gy"))
    capacity = max(2, 2 * slates * length // shards)
    owner = candidate_owner.reshape(slates * length)
    row_index = candidate_row.reshape(slates * length)
    slot = slot_numbers(owner, shards, length)
    position = owner * capacity + slot
    outgoing = jnp.full((shards * capacity,), -1, jnp.int32).at[position].set(row_index)
    outgoing = outgoing.reshape(shards, capacity)
    outer = lax.axis_size("gx")
    inner = lax.axis_size("gy")
    wanted = joined_exchange(
        outgoing.reshape(outer, inner, capacity), ("gx", "gy"), ("gx", "gy"), (0, 1), (0, 1)
    )
    found = fetch_rows(item_table, wanted)
    returned = joined_exchange(found, ("gx", "gy"), ("gx", "gy"), (0, 1), (0, 1))
    returned = returned.reshape(shards * capacity, width)
    emb = jnp.take(returned, position, axis=0).reshape(slates, length, width)
    return score_slates(emb, w_in, w_qkv, w_out, w_up, w_down, norm_gains, final_gain, w_score)


def solution(mesh):
    return jax.shard_map(
        per_device,
        mesh=mesh,
        in_specs=(
            P(("gx", "gy"), None, None),
            P(("gx", "gy"), None),
            P(("gx", "gy"), None),
            P(),
            P(),
            P(),
            P(),
            P(),
            P(),
            P(),
            P(),
        ),
        out_specs=P(("gx", "gy"), None),
        check_vma=False,
    )
```

profile of v0, /device:TPU:1, one launch (start us, length us, event | category | flops | bytes accessed | tf_op | source)
XLA Modules:
  0.0 347.7 jit_solution(3465524275925388743)
XLA Ops:
  4.1 15.5 %scatter_custom_fusion = s32[8192]{0:T(1024)S(1)} fusion(s32[4096]{0:T(1024)S(1)} %bitcast.137, s32[4096]{0:T(1024)S(1)} %bitcast.142, s32[]{:T(128)} %constant.82.clone.1), kind=kCustom, calls=%fused_computation.85 | custom fusion | bytes 32772 | tf_op jit(solution)/shard_map/scatter | solution.py:123
  19.8 21.0 %all_to_all.10 = s32[128,1,1,64]{3,2,1,0:T(1,128)S(1)} all-to-all(s32[128,1,1,64]{3,2,1,0:T(1,128)S(1)} %bitcast.131), channel_id=1, replica_groups=mesh['gx'=32,'gy'=4] {'gx','gy'}, dimensions={0} | all-to-all | bytes 65536 | tf_op jit(solution)/shard_map/all_to_all | solution.py:27
  40.9 31.1 %gather_fusion = bf16[8192,128]{1,0:T(8,128)(2,1)S(1)} fusion(bf16[78336,128]{1,0:T(8,128)(2,1)} %param.15, s32[8192]{0:T(1024)S(1)} %broadcast_clamp_fusion), kind=kCustom, calls=%fused_computation | custom fusion | bytes 4227072 | tf_op jit(solution)/shard_map/jit(_take)/gather | solution.py:97
  72.1 4.6 %select_select_fusion = bf16[128,1,1,64,128]{4,3,2,1,0:T(8,128)(2,1)} fusion(bf16[128,1,1,64,128]{4,3,2,1,0:T(8,128)(2,1)S(1)} %bitcast.126, pred[128,64]{1,0:T(8,128)(4,1)S(1)} %bitcast.134, pred[128,64]{1,0:T(8,128)(4,1)S(1)} %compare_bitcast_fusion), kind=kLoop, calls=%fused_computation.53 | loop fusion | flops 2097152 | bytes 4210688 | tf_op jit(solution)/shard_map/jit(_where)/select_n | solution.py:98
  76.7 4.3 %all-to-all-start.1 = ((bf16[128,1,1,64,128]{4,3,2,1,0:T(8,128)(2,1)}), bf16[128,1,1,64,128]{4,3,2,1,0:T(8,128)(2,1)S(1)}, u32[]{:S(2)}, u32[]{:S(2)}) async-start(bf16[128,1,1,64,128]{4,3,2,1,0:T(8,128)(2,1)} %select_select_fusion), calls=%async_computation.1 | async-start | bytes 4194304 | tf_op jit(solution)/shard_map/all_to_all | solution.py:27
  81.6 30.1 %all-to-all-done.1 = bf16[128,1,1,64,128]{4,3,2,1,0:T(8,128)(2,1)S(1)} async-done(((bf16[128,1,1,64,128]{4,3,2,1,0:T(8,128)(2,1)}), bf16[128,1,1,64,128]{4,3,2,1,0:T(8,128)(2,1)S(1)}, u32[]{:S(2)}, u32[]{:S(2)}) %all-to-all-start.1) | async-done | bytes 2097184 | tf_op jit(solution)/shard_map/all_to_all | solution.py:27
  111.7 14.9 %gather_fusion.1 = bf16[4096,128]{1,0:T(8,128)(2,1)} fusion(bf16[8192,128]{1,0:T(8,128)(2,1)S(1)} %bitcast.123, s32[4096]{0:T(1024)S(1)} %broadcast_clamp_fusion.1), kind=kCustom, calls=%fused_computation.1 | custom fusion | bytes 2113536 | tf_op jit(solution)/shard_map/jit(_take)/gather | solution.py:133
  126.6 3.7 %fusion.93 = (f32[4096]{0:T(1024)S(1)}, f32[4096,512]{0,1:T(8,128)S(1)}) fusion(bf16[128,512]{1,0:T(8,128)(2,1)S(1)} %copy-done.5, bf16[4096,128]{1,0:T(8,128)(2,1)} %gather_fusion.1, pred[4096]{0:T(1024)(128)(4,1)S(1)} %compare_and_fusion), kind=kOutput, calls=%fused_computation.104 | convolution fusion | flops 539488256 | bytes 9588736 | tf_op jit(solution)/shard_map/dot_general | solution.py:55
  130.3 1.0 multiply_reduce_fusion.4
  131.3 1.5 multiply_convert_fusion.1
  133.9 4.4 %convolution_convert_fusion.2 = bf16[4096,512]{1,0:T(8,128)(2,1)} fusion(bf16[4096,512]{0,1:T(8,128)(2,1)S(1)} %multiply_convert_fusion.1, bf16[512,1536]{1,0:T(8,128)(2,1)S(1)} %bitcast.145), kind=kOutput, calls=%fused_computation.48 | convolution fusion | flops 2149580800 | bytes 8912896 | tf_op jit(solution)/shard_map/dot_general | solution.py:64
  138.3 4.4 %convolution_convert_fusion.1 = bf16[4096,512]{1,0:T(8,128)(2,1)} fusion(bf16[4096,512]{0,1:T(8,128)(2,1)S(1)} %multiply_convert_fusion.1, bf16[512,1536]{1,0:T(8,128)(2,1)S(1)} %bitcast.146), kind=kOutput, calls=%fused_computation.47 | convolution fusion | flops 2149580800 | bytes 8912896 | tf_op jit(solution)/shard_map/dot_general | solution.py:58
  142.7 4.4 %convolution_convert_fusion = bf16[4096,512]{1,0:T(8,128)(2,1)} fusion(bf16[4096,512]{0,1:T(8,128)(2,1)S(1)} %multiply_convert_fusion.1, bf16[512,1536]{1,0:T(8,128)(2,1)S(1)} %bitcast.147), kind=kOutput, calls=%fused_computation.46 | convolution fusion | flops 2149580800 | bytes 8912896 | tf_op jit(solution)/shard_map/dot_general | solution.py:61
  147.1 11.2 %reshape.256 = bf16[8,512,8,64]{3,2,1,0:T(8,128)(2,1)} reshape(bf16[4096,512]{1,0:T(8,128)(2,1)} %convolution_convert_fusion.2) | data formatting | bytes 8388608 | tf_op jit(solution)/shard_map/reshape | solution.py:69
  158.3 9.8 %copy.42 = bf16[8,512,8,64]{1,3,2,0:T(8,128)(2,1)} copy(bf16[8,512,8,64]{3,2,1,0:T(8,128)(2,1)} %reshape.256) | data formatting | bytes 8388608 | tf_op jit(solution)/shard_map/while | solution.py:70
  168.1 11.2 %reshape.257 = bf16[8,512,8,64]{3,2,1,0:T(8,128)(2,1)} reshape(bf16[4096,512]{1,0:T(8,128)(2,1)} %convolution_convert_fusion.1) | data formatting | bytes 8388608 | tf_op jit(solution)/shard_map/reshape | solution.py:67
  179.3 9.7 %copy.43 = bf16[8,512,8,64]{1,3,2,0:T(8,128)(2,1)} copy(bf16[8,512,8,64]{3,2,1,0:T(8,128)(2,1)} %reshape.257) | data formatting | bytes 8388608 | tf_op jit(solution)/shard_map/while | solution.py:70
  189.0 11.2 %reshape.258 = bf16[8,512,8,64]{3,2,1,0:T(8,128)(2,1)} reshape(bf16[4096,512]{1,0:T(8,128)(2,1)} %convolution_convert_fusion) | data formatting | bytes 8388608 | tf_op jit(solution)/shard_map/reshape | solution.py:68
  200.2 9.7 %copy.44 = bf16[8,512,8,64]{1,3,2,0:T(8,128)(2,1)} copy(bf16[8,512,8,64]{3,2,1,0:T(8,128)(2,1)} %reshape.258) | data formatting | bytes 8388608 | tf_op jit(solution)/shard_map/while | solution.py:70
  210.0 101.8 %while.10 = (s32[]{:T(128)}, bf16[8,512,512]{2,1,0:T(8,128)(2,1)}, bf16[8,512,8,64]{1,3,2,0:T(8,128)(2,1)}, bf16[8,512,8,64]{1,3,2,0:T(8,128)(2,1)}, bf16[8,512,8,64]{1,3,2,0:T(8,128)(2,1)}, /*index=5*/s32[]{:T(128)}) while((s32[]{:T(128)}, bf16[8,512,512]{2,1,0:T(8,128)(2,1)}, bf16[8,512,8,64]{1,3,2,0:T(8,128)(2,1)}, ...), condition=%wide.region_8.9_spmd, body=%wide.region_5.8_spmd.sunk | while | flops 547619328 | bytes 21006404 | solution.py:70
  210.0 7.3 %fusion.111 = (f32[8,512]{1,0:T(8,128)S(1)}, f32[8,512,512]{1,2,0:T(8,128)}) fusion(bf16[8,512,8,64]{1,3,2,0:T(8,128)(2,1)} %get-tuple-element.126, s32[]{:T(128)} %get-tuple-element.116, bf16[8,512,8,64]{1,3,2,0:T(8,128)(2,1)} %get-tuple-element.125), kind=kOutput, calls=%fused_computation.101.clone.1 | convolution fusion | flops 274727424 | bytes 9454592 | tf_op jit(solution)/shard_map/while/body/eval_jaxpr/sub | solution.py:46
  217.3 4.4 %fusion.112 = bf16[8,64,512]{2,1,0:T(8,128)(2,1)S(1)} fusion(f32[8,512,512]{1,2,0:T(8,128)} %get-tuple-element.108, f32[8,512]{1,0:T(8,128)S(1)} %get-tuple-element.109, bf16[8,512,8,64]{1,3,2,0:T(8,128)(2,1)} %get-tuple-element.124, s32[]{:T(128)} %get-tuple-element.116), kind=kOutput, calls=%fused_computation.10.clone.1 | convolution fusion | flops 272891904 | bytes 9454080 | tf_op jit(solution)/shard_map/while/body/eval_jaxpr/hqk,khd->qhd/dot_general | solution.py:47
  221.9 0.9 constant_dynamic-update-slice_fusion.2
  222.8 7.2 %fusion.111 = (f32[8,512]{1,0:T(8,128)S(1)}, f32[8,512,512]{1,2,0:T(8,128)}) fusion(bf16[8,512,8,64]{1,3,2,0:T(8,128)(2,1)} %get-tuple-element.126, s32[]{:T(128)} %get-tuple-element.116, bf16[8,512,8,64]{1,3,2,0:T(8,128)(2,1)} %get-tuple-element.125), kind=kOutput, calls=%fused_computation.101.clone.1 | convolution fusion | flops 274727424 | bytes 9454592 | tf_op jit(solution)/shard_map/while/body/eval_jaxpr/sub | solution.py:46
  230.0 4.4 %fusion.112 = bf16[8,64,512]{2,1,0:T(8,128)(2,1)S(1)} fusion(f32[8,512,512]{1,2,0:T(8,128)} %get-tuple-element.108, f32[8,512]{1,0:T(8,128)S(1)} %get-tuple-element.109, bf16[8,512,8,64]{1,3,2,0:T(8,128)(2,1)} %get-tuple-element.124, s32[]{:T(128)} %get-tuple-element.116), kind=kOutput, calls=%fused_computation.10.clone.1 | convolution fusion | flops 272891904 | bytes 9454080 | tf_op jit(solution)/shard_map/while/body/eval_jaxpr/hqk,khd->qhd/dot_general | solution.py:47
  234.6 0.9 constant_dynamic-update-slice_fusion.2
  235.6 7.2 %fusion.111 = (f32[8,512]{1,0:T(8,128)S(1)}, f32[8,512,512]{1,2,0:T(8,128)}) fusion(bf16[8,512,8,64]{1,3,2,0:T(8,128)(2,1)} %get-tuple-element.126, s32[]{:T(128)} %get-tuple-element.116, bf16[8,512,8,64]{1,3,2,0:T(8,128)(2,1)} %get-tuple-element.125), kind=kOutput, calls=%fused_computation.101.clone.1 | convolution fusion | flops 274727424 | bytes 9454592 | tf_op jit(solution)/shard_map/while/body/eval_jaxpr/sub | solution.py:46
  242.8 4.4 %fusion.112 = bf16[8,64,512]{2,1,0:T(8,128)(2,1)S(1)} fusion(f32[8,512,512]{1,2,0:T(8,128)} %get-tuple-element.108, f32[8,512]{1,0:T(8,128)S(1)} %get-tuple-element.109, bf16[8,512,8,64]{1,3,2,0:T(8,128)(2,1)} %get-tuple-element.124, s32[]{:T(128)} %get-tuple-element.116), kind=kOutput, calls=%fused_computation.10.clone.1 | convolution fusion | flops 272891904 | bytes 9454080 | tf_op jit(solution)/shard_map/while/body/eval_jaxpr/hqk,khd->qhd/dot_general | solution.py:47
  248.2 7.2 %fusion.111 = (f32[8,512]{1,0:T(8,128)S(1)}, f32[8,512,512]{1,2,0:T(8,128)}) fusion(bf16[8,512,8,64]{1,3,2,0:T(8,128)(2,1)} %get-tuple-element.126, s32[]{:T(128)} %get-tuple-element.116, bf16[8,512,8,64]{1,3,2,0:T(8,128)(2,1)} %get-tuple-element.125), kind=kOutput, calls=%fused_computation.101.clone.1 | convolution fusion | flops 274727424 | bytes 9454592 | tf_op jit(solution)/shard_map/while/body/eval_jaxpr/sub | solution.py:46
  255.5 4.4 %fusion.112 = bf16[8,64,512]{2,1,0:T(8,128)(2,1)S(1)} fusion(f32[8,512,512]{1,2,0:T(8,128)} %get-tuple-element.108, f32[8,512]{1,0:T(8,128)S(1)} %get-tuple-element.109, bf16[8,512,8,64]{1,3,2,0:T(8,128)(2,1)} %get-tuple-element.124, s32[]{:T(128)} %get-tuple-element.116), kind=kOutput, calls=%fused_computation.10.clone.1 | convolution fusion | flops 272891904 | bytes 9454080 | tf_op jit(solution)/shard_map/while/body/eval_jaxpr/hqk,khd->qhd/dot_general | solution.py:47
  260.9 7.2 %fusion.111 = (f32[8,512]{1,0:T(8,128)S(1)}, f32[8,512,512]{1,2,0:T(8,128)}) fusion(bf16[8,512,8,64]{1,3,2,0:T(8,128)(2,1)} %get-tuple-element.126, s32[]{:T(128)} %get-tuple-element.116, bf16[8,512,8,64]{1,3,2,0:T(8,128)(2,1)} %get-tuple-element.125), kind=kOutput, calls=%fused_computation.101.clone.1 | convolution fusion | flops 274727424 | bytes 9454592 | tf_op jit(solution)/shard_map/while/body/eval_jaxpr/sub | solution.py:46
  268.2 4.4 %fusion.112 = bf16[8,64,512]{2,1,0:T(8,128)(2,1)S(1)} fusion(f32[8,512,512]{1,2,0:T(8,128)} %get-tuple-element.108, f32[8,512]{1,0:T(8,128)S(1)} %get-tuple-element.109, bf16[8,512,8,64]{1,3,2,0:T(8,128)(2,1)} %get-tuple-element.124, s32[]{:T(128)} %get-tuple-element.116), kind=kOutput, calls=%fused_computation.10.clone.1 | convolution fusion | flops 272891904 | bytes 9454080 | tf_op jit(solution)/shard_map/while/body/eval_jaxpr/hqk,khd->qhd/dot_general | solution.py:47
  272.8 0.9 constant_dynamic-update-slice_fusion.2
  273.7 7.2 %fusion.111 = (f32[8,512]{1,0:T(8,128)S(1)}, f32[8,512,512]{1,2,0:T(8,128)}) fusion(bf16[8,512,8,64]{1,3,2,0:T(8,128)(2,1)} %get-tuple-element.126, s32[]{:T(128)} %get-tuple-element.116, bf16[8,512,8,64]{1,3,2,0:T(8,128)(2,1)} %get-tuple-element.125), kind=kOutput, calls=%fused_computation.101.clone.1 | convolution fusion | flops 274727424 | bytes 9454592 | tf_op jit(solution)/shard_map/while/body/eval_jaxpr/sub | solution.py:46
  280.9 4.4 %fusion.112 = bf16[8,64,512]{2,1,0:T(8,128)(2,1)S(1)} fusion(f32[8,512,512]{1,2,0:T(8,128)} %get-tuple-element.108, f32[8,512]{1,0:T(8,128)S(1)} %get-tuple-element.109, bf16[8,512,8,64]{1,3,2,0:T(8,128)(2,1)} %get-tuple-element.124, s32[]{:T(128)} %get-tuple-element.116), kind=kOutput, calls=%fused_computation.10.clone.1 | convolution fusion | flops 272891904 | bytes 9454080 | tf_op jit(solution)/shard_map/while/body/eval_jaxpr/hqk,khd->qhd/dot_general | solution.py:47
  285.5 0.9 constant_dynamic-update-slice_fusion.2
  286.4 7.2 %fusion.111 = (f32[8,512]{1,0:T(8,128)S(1)}, f32[8,512,512]{1,2,0:T(8,128)}) fusion(bf16[8,512,8,64]{1,3,2,0:T(8,128)(2,1)} %get-tuple-element.126, s32[]{:T(128)} %get-tuple-element.116, bf16[8,512,8,64]{1,3,2,0:T(8,128)(2,1)} %get-tuple-element.125), kind=kOutput, calls=%fused_computation.101.clone.1 | convolution fusion | flops 274727424 | bytes 9454592 | tf_op jit(solution)/shard_map/while/body/eval_jaxpr/sub | solution.py:46
  293.6 4.4 %fusion.112 = bf16[8,64,512]{2,1,0:T(8,128)(2,1)S(1)} fusion(f32[8,512,512]{1,2,0:T(8,128)} %get-tuple-element.108, f32[8,512]{1,0:T(8,128)S(1)} %get-tuple-element.109, bf16[8,512,8,64]{1,3,2,0:T(8,128)(2,1)} %get-tuple-element.124, s32[]{:T(128)} %get-tuple-element.116), kind=kOutput, calls=%fused_computation.10.clone.1 | convolution fusion | flops 272891904 | bytes 9454080 | tf_op jit(solution)/shard_map/while/body/eval_jaxpr/hqk,khd->qhd/dot_general | solution.py:47
  299.1 7.2 %fusion.111 = (f32[8,512]{1,0:T(8,128)S(1)}, f32[8,512,512]{1,2,0:T(8,128)}) fusion(bf16[8,512,8,64]{1,3,2,0:T(8,128)(2,1)} %get-tuple-element.126, s32[]{:T(128)} %get-tuple-element.116, bf16[8,512,8,64]{1,3,2,0:T(8,128)(2,1)} %get-tuple-element.125), kind=kOutput, calls=%fused_computation.101.clone.1 | convolution fusion | flops 274727424 | bytes 9454592 | tf_op jit(solution)/shard_map/while/body/eval_jaxpr/sub | solution.py:46
  306.3 4.4 %fusion.112 = bf16[8,64,512]{2,1,0:T(8,128)(2,1)S(1)} fusion(f32[8,512,512]{1,2,0:T(8,128)} %get-tuple-element.108, f32[8,512]{1,0:T(8,128)S(1)} %get-tuple-element.109, bf16[8,512,8,64]{1,3,2,0:T(8,128)(2,1)} %get-tuple-element.124, s32[]{:T(128)} %get-tuple-element.116), kind=kOutput, calls=%fused_computation.10.clone.1 | convolution fusion | flops 272891904 | bytes 9454080 | tf_op jit(solution)/shard_map/while/body/eval_jaxpr/hqk,khd->qhd/dot_general | solution.py:47
  310.9 0.8 constant_dynamic-update-slice_fusion.2
  311.8 7.1 %fusion.94 = (f32[4096]{0:T(1024)S(1)}, f32[4096,512]{0,1:T(8,128)S(1)}) fusion(f32[4096,512]{0,1:T(8,128)} %copy-done.1, bf16[4096,512]{1,0:T(8,128)(2,1)} %bitcast.125, bf16[1,512,512]{2,1,0:T(8,128)(2,1)S(1)} %copy-done.4), kind=kOutput, calls=%fused_computation.105 | convolution fusion | flops 2151673856 | bytes 21512192 | tf_op jit(solution)/shard_map/dot_general | solution.py:71
  318.9 3.2 copy-done.2
  322.1 1.0 multiply_reduce_fusion.3
  323.1 15.8 %fusion.95 = (f32[4096]{0:T(1024)S(1)}, f32[4096,512]{0,1:T(8,128)}) fusion(f32[4096,512]{0,1:T(8,128)} %copy-done.2, bf16[1,1024,512]{2,1,0:T(8,128)(2,1)S(1)} %copy-done, f32[512]{0:T(512)S(1)} %bitcast.144, f32[4096]{0:T(1024)S(1)} %add_rsqrt_fusion.1, f32[4096]{0:T(1024)S(1)} %broadcast_multiply_fusion.1, bf16[1,512,1024]{2,1,0:T(8,128)(2,1)S(1)} %copy-done.11), kind=kOutput, calls=%fused_computation.106 | convolution fusion | flops 8640262144 | bytes 18925568 | tf_op jit(solution)/shard_map/dot_general | solution.py:76
  338.9 4.5 %multiply_reduce_fusion.2 = f32[4096]{0:T(1024)S(1)} fusion(f32[4096,512]{0,1:T(8,128)} %get-tuple-element.74, f32[4096]{0:T(1024)S(1)} %broadcast_multiply_fusion), kind=kLoop, calls=%fused_computation.38 | loop fusion | flops 6287360 | bytes 8421376 | tf_op jit(solution)/shard_map/reduce_sum | solution.py:35
  343.5 1.2 copy-done.3
  344.7 2.0 multiply_reduce_fusion.1
  (65 shorter events, 11.2 us)
Async XLA Ops:
  0.0 323.1 %copy-start = (bf16[1,1024,512]{2,1,0:T(8,128)(2,1)S(1)}, bf16[1,1024,512]{2,1,0:T(8,128)(2,1)}, u32[]{:S(2)}) copy-start(bf16[1,1024,512]{2,1,0:T(8,128)(2,1)} %param.20) | copy-start | bytes 3145732
  72.1 8.9 %copy-start.9 = (bf16[512]{0:T(512)(128)(2,1)S(1)}, bf16[512]{0:T(512)(128)(2,1)}, u32[]{:S(2)}) copy-start(bf16[512]{0:T(512)(128)(2,1)} %param.23) | copy-start | bytes 3076
  72.1 9.5 %copy-start.7 = (f32[1,2,512]{2,1,0:T(2,128)S(1)}, f32[1,2,512]{2,1,0:T(2,128)}, u32[]{:S(2)}) copy-start(f32[1,2,512]{2,1,0:T(2,128)} %param.21) | copy-start | bytes 12292
  72.1 54.5 %copy-start.5 = (bf16[128,512]{1,0:T(8,128)(2,1)S(1)}, bf16[128,512]{1,0:T(8,128)(2,1)}, u32[]{:S(2)}) copy-start(bf16[128,512]{1,0:T(8,128)(2,1)} %param.16) | copy-start | bytes 393220
  76.7 35.0 %all-to-all-start.1 = ((bf16[128,1,1,64,128]{4,3,2,1,0:T(8,128)(2,1)}), bf16[128,1,1,64,128]{4,3,2,1,0:T(8,128)(2,1)S(1)}, u32[]{:S(2)}, u32[]{:S(2)}) async-start(bf16[128,1,1,64,128]{4,3,2,1,0:T(8,128)(2,1)} %select_select_fusion), calls=%async_computation.1 | async-start | bytes 4194304 | tf_op jit(solution)/shard_map/all_to_all | solution.py:27
  130.3 3.4 copy-start.1
  131.3 2.6 copy-start.10
  210.0 101.8 %copy-start.4 = (bf16[1,512,512]{2,1,0:T(8,128)(2,1)S(1)}, bf16[1,512,512]{2,1,0:T(8,128)(2,1)}, u32[]{:S(2)}) copy-start(bf16[1,512,512]{2,1,0:T(8,128)(2,1)} %param.18) | copy-start | bytes 1572868
  318.9 3.2 copy-start.2
  318.9 4.2 %copy-start.11 = (bf16[1,512,1024]{2,1,0:T(8,128)(2,1)S(1)}, bf16[1,512,1024]{2,1,0:T(8,128)(2,1)}, u32[]{:S(2)}) copy-start(bf16[1,512,1024]{2,1,0:T(8,128)(2,1)} %param.19) | copy-start | bytes 3145732
  338.9 5.8 %copy-start.3 = (f32[4096,512]{0,1:T(8,128)S(1)}, f32[4096,512]{0,1:T(8,128)}, u32[]{:S(2)}) copy-start(f32[4096,512]{0,1:T(8,128)} %get-tuple-element.74) | copy-start | bytes 25165828
  338.9 5.8 %copy-start.6 = (f32[512]{0:T(512)S(1)}, f32[512]{0:T(512)}, u32[]{:S(2)}) copy-start(f32[512]{0:T(512)} %convert_element_type.67) | copy-start | bytes 6148
  338.9 5.8 %copy-start.8 = (f32[512]{0:T(512)S(1)}, f32[512]{0:T(512)}, u32[]{:S(2)}) copy-start(f32[512]{0:T(512)} %param.22) | copy-start | bytes 6148
where the time goes:
time: 350 us; the launch traced here: 348 us
  local copies, waits for them, and re-layouts  140 us (40%)
  matrix products  134 us (38%)
  waiting for transfers between devices  30.1 us (9%)
  blocking collectives  21 us (6%)
  other arithmetic  18 us (5%)
  starting transfers between devices  4.26 us (1%)
    sub x8, matrix products, attend_slate(): probs = jax.nn.softmax(scores, axis=-1).astype(jnp.bfloat16)  57.8 us
    dot_general x8, matrix products, attend_slate(): jnp.einsum('hqk,khd->qhd', probs, values, preferred_element_type=jnp.floa...  35.3 us
    gather x1, local copies, waits for them, and re-layouts, fetch_rows(): rows = jnp.take(item_table, jnp.maximum(flat, 0), axis=0)  31.1 us
    all_to_all x1, waiting for transfers between devices, joined_exchange(): parts = lax.all_to_all(parts, axis, split_axis=0, concat_axis=0, tiled=True)  30.1 us
    while x3, local copies, waits for them, and re-layouts, score_slates(): lax.map(attend_slate, (query, keys, values)).reshape(slates * length, model)  29.2 us
    all_to_all x1, blocking collectives, joined_exchange(): parts = lax.all_to_all(parts, axis, split_axis=0, concat_axis=0, tiled=True)  21 us
    dot_general x1, matrix products, score_slates(): jnp.dot(inner, w_down[0], preferred_element_type=jnp.float32)  15.8 us
    scatter x1, local copies, waits for them, and re-layouts, per_device(): jnp.full((shards * capacity,), -1, jnp.int32).at[position].set(row_index)  15.5 us
  transfers between devices with their start and end apart: 1, of which 1 were waited for; matrix products, arithmetic and copies ran while one was open for 0% of the time, Pallas kernels for 0%

commit v1 on v0

v1 whole, which is shorter than its diff:
```python
import functools

import jax
import jax.numpy as jnp
from jax import lax
from jax.experimental import pallas as pl
from jax.experimental.pallas import tpu as pltpu
from jax.sharding import PartitionSpec as P

HEADS = 8
MESH = pl.DeviceIdType.MESH


def layer_norm(values, gain):
    mean = jnp.mean(values, axis=-1, keepdims=True)
    centred = values - mean
    variance = jnp.mean(centred * centred, axis=-1, keepdims=True)
    return centred * lax.rsqrt(variance + 1e-05) * gain


def slate_kernel(
    emb_ref, w_in_ref, w_qkv_ref, w_out_ref, w_up_ref, w_down_ref, gains_ref, final_ref, score_ref,
    out_ref, qkv_ref, mixed_ref,
):
    length, model = mixed_ref.shape
    resid = jnp.dot(emb_ref[...], w_in_ref[...], preferred_element_type=jnp.float32)
    normed = layer_norm(resid, gains_ref[0:1, :]).astype(jnp.bfloat16)
    qkv_ref[...] = jnp.dot(normed, w_qkv_ref[...], preferred_element_type=jnp.float32).astype(
        jnp.bfloat16
    )
    low = lax.broadcasted_iota(jnp.int32, (1, 128), 1) < 64
    scales = (
        jnp.where(low, 0.125, 0.0).astype(jnp.bfloat16),
        jnp.where(low, 0.0, 0.125).astype(jnp.bfloat16),
    )
    ones = jnp.ones((length, 128), jnp.bfloat16)
    for first in range(0, model, 128):
        query = qkv_ref[:, first : first + 128]
        keys = qkv_ref[:, model + first : model + first + 128]
        values = qkv_ref[:, 2 * model + first : 2 * model + first + 128]
        values = jnp.concatenate([values, ones], axis=1)
        heads = []
        for scale in scales:
            scores = lax.dot_general(
                query * scale, keys, (((1,), (1,)), ((), ())), preferred_element_type=jnp.float32
            )
            top = jnp.max(scores, axis=-1, keepdims=True)
            weights = jnp.exp(scores - top).astype(jnp.bfloat16)
            both = jnp.dot(weights, values, preferred_element_type=jnp.float32)
            heads.append(both[:, :128] / both[:, 128:])
        mixed_ref[:, first : first + 128] = jnp.where(low, heads[0], heads[1]).astype(jnp.bfloat16)
    resid = resid + jnp.dot(mixed_ref[...], w_out_ref[...], preferred_element_type=jnp.float32)
    normed = layer_norm(resid, gains_ref[1:2, :]).astype(jnp.bfloat16)
    inner = jax.nn.gelu(
        jnp.dot(normed, w_up_ref[...], preferred_element_type=jnp.float32)
    ).astype(jnp.bfloat16)
    resid = resid + jnp.dot(inner, w_down_ref[...], preferred_element_type=jnp.float32)
    final = layer_norm(resid, final_ref[...])
    logits = jnp.sum(final * score_ref[...].astype(jnp.float32), axis=-1).reshape(1, length)
    shifted = logits - jnp.max(logits, axis=-1, keepdims=True)
    total = jnp.sum(jnp.exp(shifted), axis=-1, keepdims=True)
    out_ref[...] = (shifted - jnp.log(total))[None]


def score_slates(emb, w_in, w_qkv, w_out, w_up, w_down, norm_gains, final_gain, w_score):
    slates, length, width = emb.shape
    model = w_in.shape[1]
    whole = (
        w_in, w_qkv[0], w_out[0], w_up[0], w_down[0], norm_gains[0], final_gain[None], w_score[None],
    )
    scored = pl.pallas_call(
        slate_kernel,
        grid=(slates,),
        in_specs=[pl.BlockSpec((length, width), lambda i: (i, 0))]
        + [pl.BlockSpec(a.shape, lambda i: (0, 0)) for a in whole],
        out_specs=pl.BlockSpec((1, 1, length), lambda i: (i, 0, 0)),
        out_shape=jax.ShapeDtypeStruct((slates, 1, length), jnp.float32),
        scratch_shapes=[
            pltpu.VMEM((length, 3 * model), jnp.bfloat16),
            pltpu.VMEM((length, model), jnp.bfloat16),
        ],
        compiler_params=pltpu.CompilerParams(vmem_limit_bytes=40 * 1024 * 1024),
        name="slates",
    )(emb.reshape(slates * length, width), *whole)
    return scored.reshape(slates, length)


def slot_numbers(owner, shards, length):
    total = owner.shape[0]
    onehot = (owner[:, None] == jnp.arange(shards, dtype=jnp.int32)[None, :]).astype(jnp.bfloat16)
    blocks = onehot.reshape(total // length, length, shards)
    lower = (jnp.arange(length)[:, None] >= jnp.arange(length)[None, :]).astype(jnp.bfloat16)
    within = jnp.einsum("ij,bjn->bin", lower, blocks, preferred_element_type=jnp.float32)
    totals = within[:, -1, :]
    before = jnp.cumsum(totals, axis=0) - totals
    counts = within + before[:, None, :]
    picked = jnp.sum(counts * blocks.astype(jnp.float32), axis=-1)
    return (picked.reshape(total) - 1.0).astype(jnp.int32)


def peer(step):
    gx, gy = lax.axis_index("gx"), lax.axis_index("gy")
    x, y, core = gx // 8, (gx // 2) % 4, gx % 2
    to_x, to_y = (x + step % 4) % 4, (y + (step // 4) % 4) % 4
    to_z, to_core = (gy + (step // 16) % 4) % 4, (core + step // 64) % 2
    to_gx = (to_x * 4 + to_y) * 2 + to_core
    return to_gx, to_z, to_gx * 4 + to_z


def exchange_kernel(
    want_ref, table_ref, out_ref, packed, table, block, sending, asked, numbers,
    chunk_sems, ask_send, ask_recv, row_send, row_recv, number_sem, *, shards, chunks, capacity,
):
    length = table_ref.shape[0] // chunks
    me = lax.axis_index("gx") * 4 + lax.axis_index("gy")

    def chunk_copy(chunk):
        piece = pl.ds(chunk * length, length)
        return pltpu.make_async_copy(table_ref.at[piece], packed.at[piece], chunk_sems.at[chunk])

    for chunk in range(chunks):
        chunk_copy(chunk).start()
    barrier = pltpu.get_barrier_semaphore()

    def greet(step, carry):
        to_gx, to_gy, _ = peer(step)
        pl.semaphore_signal(barrier, inc=1, device_id=(to_gx, to_gy), device_id_type=MESH)
        return carry

    lax.fori_loop(1, shards, greet, 0)
    pl.semaphore_wait(barrier, shards - 1)

    def ask(step, carry):
        to_gx, to_gy, shard = peer(step)
        pltpu.make_async_remote_copy(
            src_ref=want_ref.at[shard], dst_ref=asked.at[me], send_sem=ask_send, recv_sem=ask_recv,
            device_id=(to_gx, to_gy), device_id_type=MESH,
        ).start()
        return carry

    lax.fori_loop(1, shards, ask, 0)
    asked[pl.ds(me, 1)] = want_ref[pl.ds(me, 1)]
    for chunk in range(chunks):
        chunk_copy(chunk).wait()

        def widen(part, carry):
            piece = pl.ds(chunk * length + part * 128, 128)
            table[piece] = packed[piece].astype(jnp.float32)
            return carry

        lax.fori_loop(0, length // 128, widen, 0)
    others = pl.ds(0, shards - 1)
    pltpu.make_async_copy(asked.at[others], asked.at[others], ask_recv).wait()
    pltpu.make_async_copy(asked.at[others], asked.at[others], ask_send).wait()
    copy = pltpu.make_async_copy(asked, numbers, number_sem)
    copy.start()
    copy.wait()

    def collect(shard, target):
        for slot in range(capacity):
            block[pl.ds(slot, 1)] = table[pl.ds(numbers[shard, 0, slot], 1)]
        target[...] = block[...].astype(jnp.bfloat16)

    def give(step, carry):
        to_gx, to_gy, shard = peer(step)
        collect(shard, sending.at[shard])
        pltpu.make_async_remote_copy(
            src_ref=sending.at[shard], dst_ref=out_ref.at[me], send_sem=row_send, recv_sem=row_recv,
            device_id=(to_gx, to_gy), device_id_type=MESH,
        ).start()
        return carry

    lax.fori_loop(1, shards, give, 0)
    collect(me, out_ref.at[me])
    pltpu.make_async_copy(out_ref.at[others], out_ref.at[others], row_recv).wait()
    pltpu.make_async_copy(out_ref.at[others], out_ref.at[others], row_send).wait()


def exchange(want, item_table, capacity):
    shards, _, lanes = want.shape
    rows, width = item_table.shape
    chunks = 6
    return pl.pallas_call(
        functools.partial(exchange_kernel, shards=shards, chunks=chunks, capacity=capacity),
        in_specs=[pl.BlockSpec(memory_space=pltpu.VMEM), pl.BlockSpec(memory_space=pl.ANY)],
        out_specs=pl.BlockSpec(memory_space=pltpu.VMEM),
        out_shape=jax.ShapeDtypeStruct((shards, capacity, width), jnp.bfloat16),
        scratch_shapes=[
            pltpu.VMEM((rows, width), jnp.bfloat16),
            pltpu.VMEM((rows, width), jnp.float32),
            pltpu.VMEM((capacity, width), jnp.float32),
            pltpu.VMEM((shards, capacity, width), jnp.bfloat16),
            pltpu.VMEM((shards, 1, lanes), jnp.int32),
            pltpu.SMEM((shards, 1, lanes), jnp.int32),
            pltpu.SemaphoreType.DMA((chunks,)),
            pltpu.SemaphoreType.DMA,
            pltpu.SemaphoreType.DMA,
            pltpu.SemaphoreType.DMA,
            pltpu.SemaphoreType.DMA,
            pltpu.SemaphoreType.DMA,
        ],
        compiler_params=pltpu.CompilerParams(
            collective_id=0, has_side_effects=True, vmem_limit_bytes=67043328
        ),
        name="exchange",
    )(want, item_table)


def per_device(
    candidate_owner,
    candidate_row,
    item_table,
    w_in,
    w_qkv,
    w_out,
    w_up,
    w_down,
    norm_gains,
    final_gain,
    w_score,
):
    slates, length, unused = candidate_owner.shape
    width = item_table.shape[1]
    shards = lax.axis_size(("gx", "gy"))
    capacity = max(2, 2 * slates * length // shards)
    owner = candidate_owner.reshape(slates * length)
    row_index = candidate_row.reshape(slates * length)
    slot = slot_numbers(owner, shards, length)
    lanes = 128
    wanted = jnp.zeros((shards * lanes,), jnp.int32).at[owner * lanes + slot].set(row_index)
    returned = exchange(wanted.reshape(shards, 1, lanes), item_table, capacity)
    returned = returned.reshape(shards * capacity, width)
    position = owner * capacity + slot
    emb = jnp.take(returned, position, axis=0).reshape(slates, length, width)
    return score_slates(emb, w_in, w_qkv, w_out, w_up, w_down, norm_gains, final_gain, w_score)


def solution(mesh):
    return jax.shard_map(
        per_device,
        mesh=mesh,
        in_specs=(
            P(("gx", "gy"), None, None),
            P(("gx", "gy"), None),
            P(("gx", "gy"), None),
            P(),
            P(),
            P(),
            P(),
            P(),
            P(),
            P(),
            P(),
        ),
        out_specs=P(("gx", "gy"), None),
        check_vma=False,
    )
```

time: 350 us -> 152 us (0.43)
  matrix products: 134 us -> 0.76 us
  Pallas kernels: 0 us -> 111 us
  local copies, waits for them, and re-layouts: 140 us -> 34.5 us
  waiting for transfers between devices: 30.1 us -> 0 us
  blocking collectives: 21 us -> 0 us
  other arithmetic: 18 us -> 5.18 us
  starting transfers between devices: 4.26 us -> 0 us
    pallas_call x0 -> x2, Pallas kernels: none -> 111 us  [the longest x1 59.3 us: exchange(): pl.pallas_call(functools.partial(exchange_kernel, shards=shards, chunks=c...]
    dot_general x14 -> x0, matrix products: 75.1 us -> none  [the longest x8 35.3 us: attend_slate(): jnp.einsum('hqk,khd->qhd', probs, values, preferred_element_type=jnp.floa...]
    sub x8 -> x0, matrix products: 57.8 us -> none  [attend_slate(): probs = jax.nn.softmax(scores, axis=-1).astype(jnp.bfloat16)]
    reshape x4 -> x0, local copies, waits for them, and re-layouts: 33.6 us -> none  [the longest x1 11.2 us: score_slates(): query = query.reshape(slates, length, HEADS, head_dim)]
    gather x1 -> x0, local copies, waits for them, and re-layouts: 31.1 us -> none  [fetch_rows(): rows = jnp.take(item_table, jnp.maximum(flat, 0), axis=0)]
    all_to_all x1 -> x0, waiting for transfers between devices: 30.1 us -> none  [joined_exchange(): parts = lax.all_to_all(parts, axis, split_axis=0, concat_axis=0, tiled=True)]
    while x3 -> x0, local copies, waits for them, and re-layouts: 29.2 us -> none  [score_slates(): lax.map(attend_slate, (query, keys, values)).reshape(slates * length, model)]
    all_to_all x1 -> x0, blocking collectives: 21 us -> none  [joined_exchange(): parts = lax.all_to_all(parts, axis, split_axis=0, concat_axis=0, tiled=True)]
  transfers between devices with their start and end apart: 1 -> 0, of which waited for: 1 -> 0; matrix products, arithmetic and copies ran while one was open for 0% -> 0% of each run, Pallas kernels for 0% -> 0%
where the time goes in v1:
time: 152 us
  Pallas kernels  111 us (73%)
  local copies, waits for them, and re-layouts  34.5 us (23%)
  other arithmetic  5.18 us (3%)
    pallas_call x1, Pallas kernels, exchange(): pl.pallas_call(functools.partial(exchange_kernel, shards=shards, chunks=c...  59.3 us
    pallas_call x1, Pallas kernels, score_slates(): pl.pallas_call(slate_kernel, grid=(slates,), in_specs=[pl.BlockSpec((leng...  51.8 us
    scatter x1, local copies, waits for them, and re-layouts, per_device(): jnp.zeros((shards * lanes,), jnp.int32).at[owner * lanes + slot]  16.1 us
    gather x1, local copies, waits for them, and re-layouts, per_device(): emb = jnp.take(returned, position, axis=0).reshape(slates, length, width)  15 us

profile of v1, /device:TPU:1, one launch (start us, length us, event | category | flops | bytes accessed | tf_op | source)
XLA Modules:
  0.0 151.7 jit_solution(9606139167501800560)
XLA Ops:
  0.0 1.3 broadcast_in_dim.28.score_ref
  1.3 0.7 copy.16
  2.0 0.7 copy.20
  2.7 0.7 broadcast_multiply_fusion.1
  3.4 0.8 fusion.2
  4.2 0.5 fusion.9
  4.7 0.5 multiply_reduce_fusion
  5.3 0.6 compare_and_fusion
  5.9 0.6 broadcast_clamp_fusion
  6.6 16.1 %scatter_custom_fusion = s32[16384]{0:T(1024)} fusion(s32[4096]{0:T(1024)S(1)} %bitcast.51, s32[4096]{0:T(1024)S(1)} %bitcast.53, s32[]{:T(128)} %constant.13.clone.1), kind=kCustom, calls=%fused_computation.16 | custom fusion | bytes 65540 | tf_op jit(solution)/shard_map/scatter | solution.py:230
  22.7 59.3 %exchange.1 = bf16[128,64,128]{2,1,0:T(8,128)(2,1)} custom-call(s32[128,1,128]{2,1,0:T(1,128)} %bitcast.42, bf16[78336,128]{1,0:T(8,128)(2,1)} %table_ref.1), custom_call_target="tpu_custom_call" | custom-call | tf_op jit(solution)/shard_map/exchange/pallas_call | solution.py:183
  81.9 0.0 copy-start.8
  81.9 0.0 copy-start.1
  82.0 0.0 copy-start.2
  82.0 0.0 copy-start.4
  82.0 0.0 copy-start.6
  82.0 15.0 %gather_fusion = bf16[4096,128]{1,0:T(8,128)(2,1)S(1)} fusion(bf16[8192,128]{1,0:T(8,128)(2,1)} %bitcast.41, s32[4096]{0:T(1024)} %broadcast_clamp_fusion), kind=kCustom, calls=%fused_computation | custom fusion | bytes 2113536 | tf_op jit(solution)/shard_map/jit(_take)/gather | solution.py:234
  97.0 0.0 copy-done.8
  97.0 0.0 copy-start
  97.0 0.0 copy-start.3
  97.0 0.0 copy-start.5
  97.0 0.0 copy-start.7
  97.0 2.1 %broadcast_select_fusion.emb_ref = bf16[4096,128]{1,0:T(8,128)(2,1)S(1)} fusion(bf16[4096,128]{1,0:T(8,128)(2,1)S(1)} %gather_fusion, pred[4096]{0:T(1024)(128)(4,1)S(1)} %copy-done.8), kind=kLoop, calls=%fused_computation.10 | loop fusion | flops 524288 | bytes 2101248 | tf_op jit(solution)/shard_map/jit(_take)/select_n | solution.py:234
  99.2 0.0 copy-done.1
  99.2 0.0 copy-done.2
  99.2 0.0 copy-done.4
  99.2 0.0 copy-done.6
  99.2 0.0 copy-done
  99.3 0.0 copy-done.3
  99.3 0.0 copy-done.5
  99.3 0.0 copy-done.7
  99.3 51.8 %slates.1 = f32[8,1,512]{2,1,0:T(1,128)S(1)} custom-call(bf16[4096,128]{1,0:T(8,128)(2,1)S(1)} %broadcast_select_fusion.emb_ref, bf16[128,512]{1,0:T(8,128)(2,1)S(1)} %copy-done.4, bf16[512,1536]{1,0:T(8,128)(2,1)S(1)} %bitcast.35, bf16[512,512]{1,0:T(8,128)(2,1)S(1)} %bitcast.38, bf16[512,1024]{1,0:T(8,128)(2,1)S(1)} %bitcast.36, ...), custom_call_target="tpu_custom_call" | custom-call | tf_op jit(solution)/shard_map/slates/pallas_call | solution.py:71
  151.1 0.6 copy.19
  (4 shorter events, 0.1 us)
Async XLA Ops:
  81.9 15.1 %copy-start.8 = (pred[4096]{0:T(1024)(128)(4,1)S(1)}, pred[4096]{0:T(1024)(128)(4,1)}, u32[]{:S(2)}) copy-start(pred[4096]{0:T(1024)(128)(4,1)} %compare_and_fusion) | copy-start | bytes 12292
  81.9 17.3 %copy-start.1 = (bf16[1,512,1024]{2,1,0:T(8,128)(2,1)S(1)}, bf16[1,512,1024]{2,1,0:T(8,128)(2,1)}, u32[]{:S(2)}) copy-start(bf16[1,512,1024]{2,1,0:T(8,128)(2,1)} %param.17) | copy-start | bytes 3145732
  82.0 17.3 %copy-start.2 = (bf16[1,1024,512]{2,1,0:T(8,128)(2,1)S(1)}, bf16[1,1024,512]{2,1,0:T(8,128)(2,1)}, u32[]{:S(2)}) copy-start(bf16[1,1024,512]{2,1,0:T(8,128)(2,1)} %param.18) | copy-start | bytes 3145732
  82.0 17.3 %copy-start.4 = (bf16[128,512]{1,0:T(8,128)(2,1)S(1)}, bf16[128,512]{1,0:T(8,128)(2,1)}, u32[]{:S(2)}) copy-start(bf16[128,512]{1,0:T(8,128)(2,1)} %w_in_ref.1) | copy-start | bytes 393220
  82.0 17.3 %copy-start.6 = (f32[1,2,512]{2,1,0:T(2,128)S(1)}, f32[1,2,512]{2,1,0:T(2,128)}, u32[]{:S(2)}) copy-start(f32[1,2,512]{2,1,0:T(2,128)} %param.19) | copy-start | bytes 12292
  97.0 2.2 %copy-start = (bf16[1,512,1536]{2,1,0:T(8,128)(2,1)S(1)}, bf16[1,512,1536]{2,1,0:T(8,128)(2,1)}, u32[]{:S(2)}) copy-start(bf16[1,512,1536]{2,1,0:T(8,128)(2,1)} %param.15) | copy-start | bytes 4718596
  97.0 2.2 %copy-start.3 = (bf16[1,512,512]{2,1,0:T(8,128)(2,1)S(1)}, bf16[1,512,512]{2,1,0:T(8,128)(2,1)}, u32[]{:S(2)}) copy-start(bf16[1,512,512]{2,1,0:T(8,128)(2,1)} %param.16) | copy-start | bytes 1572868
  97.0 2.2 %copy-start.5 = (bf16[1,512]{1,0:T(2,128)(2,1)S(1)}, bf16[1,512]{1,0:T(2,128)(2,1)}, u32[]{:S(2)}) copy-start(bf16[1,512]{1,0:T(2,128)(2,1)} %broadcast_in_dim.28.score_ref) | copy-start | bytes 3076
  97.0 2.2 %copy-start.7 = (f32[512]{0:T(512)S(1)}, f32[512]{0:T(512)}, u32[]{:S(2)}) copy-start(f32[512]{0:T(512)} %param.20) | copy-start | bytes 6148

commit v2 on v1

v2 whole, which is shorter than its diff:
```python
import functools

import jax
import jax.numpy as jnp
from jax import lax
from jax.experimental import pallas as pl
from jax.experimental.pallas import tpu as pltpu
from jax.sharding import PartitionSpec as P

MESH = pl.DeviceIdType.MESH


def layer_norm(values, gain):
    mean = jnp.mean(values, axis=-1, keepdims=True)
    centred = values - mean
    variance = jnp.mean(centred * centred, axis=-1, keepdims=True)
    return centred * lax.rsqrt(variance + 1e-05) * gain


def slate_kernel(
    place_ref, rows_ref, w_in_ref, w_qkv_ref, w_out_ref, w_up_ref, w_down_ref, gains_ref, final_ref,
    score_ref, out_ref, qkv_ref, mixed_ref, wide_ref, emb_ref, *, block,
):
    length, model = mixed_ref.shape
    step = pl.program_id(0)
    now, later = step % 2, (step + 1) % 2
    following = jnp.minimum(step + 1, pl.num_programs(0) - 1)

    @pl.when(step == 0)
    def _():
        def widen(part, carry):
            piece = pl.ds(pl.multiple_of(part * 128, 128), 128)
            wide_ref[piece] = rows_ref[piece].astype(jnp.float32)
            return carry

        lax.fori_loop(0, rows_ref.shape[0] // 128, widen, 0)

        def fetch(part, carry):
            first = pl.multiple_of(part * 32, 32)
            for r in range(32):
                emb_ref[0, pl.ds(first + r, 1)] = wide_ref[pl.ds(place_ref[0, 0, first + r], 1)]
            return carry

        lax.fori_loop(0, length // 32, fetch, 0)

    emb = emb_ref[now].astype(jnp.bfloat16)
    resid = jnp.dot(emb, w_in_ref[...], preferred_element_type=jnp.float32)
    normed = layer_norm(resid, gains_ref[0:1, :]).astype(jnp.bfloat16)
    qkv_ref[...] = jnp.dot(normed, w_qkv_ref[...], preferred_element_type=jnp.float32).astype(
        jnp.bfloat16
    )
    low = lax.broadcasted_iota(jnp.int32, (1, 128), 1) < 64
    scales = (
        jnp.where(low, 0.125, 0.0).astype(jnp.bfloat16),
        jnp.where(low, 0.0, 0.125).astype(jnp.bfloat16),
    )
    ones = jnp.ones((length, 128), jnp.bfloat16)
    pieces = [(column, row) for column in range(0, model, 128) for row in range(0, length, block)]
    share = length // len(pieces)
    for part, (column, row) in enumerate(pieces):
        for r in range(part * share, (part + 1) * share):
            emb_ref[later, pl.ds(r, 1)] = wide_ref[pl.ds(place_ref[following, 0, r], 1)]
        query = qkv_ref[row : row + block, column : column + 128]
        keys = qkv_ref[:, model + column : model + column + 128]
        values = qkv_ref[:, 2 * model + column : 2 * model + column + 128]
        values = jnp.concatenate([values, ones], axis=1)
        heads = []
        for scale in scales:
            scores = lax.dot_general(
                query * scale, keys, (((1,), (1,)), ((), ())), preferred_element_type=jnp.float32
            )
            top = jnp.max(scores, axis=-1, keepdims=True)
            weights = jnp.exp(scores - top).astype(jnp.bfloat16)
            heads.append(jnp.dot(weights, values, preferred_element_type=jnp.float32))
        sums = jnp.where(low, heads[0][:, 128:], heads[1][:, 128:])
        mixed = jnp.where(low, heads[0][:, :128], heads[1][:, :128]) / sums
        mixed_ref[row : row + block, column : column + 128] = mixed.astype(jnp.bfloat16)
    resid = resid + jnp.dot(mixed_ref[...], w_out_ref[...], preferred_element_type=jnp.float32)
    normed = layer_norm(resid, gains_ref[1:2, :]).astype(jnp.bfloat16)
    inner = jax.nn.gelu(
        jnp.dot(normed, w_up_ref[...], preferred_element_type=jnp.float32)
    ).astype(jnp.bfloat16)
    resid = resid + jnp.dot(inner, w_down_ref[...], preferred_element_type=jnp.float32)
    final = layer_norm(resid, final_ref[...])
    logits = jnp.sum(final * score_ref[...].astype(jnp.float32), axis=-1).reshape(1, length)
    shifted = logits - jnp.max(logits, axis=-1, keepdims=True)
    total = jnp.sum(jnp.exp(shifted), axis=-1, keepdims=True)
    out_ref[...] = (shifted - jnp.log(total))[None]


def score_slates(rows, place, w_in, w_qkv, w_out, w_up, w_down, norm_gains, final_gain, w_score):
    slates, _, length = place.shape
    model = w_in.shape[1]
    whole = (
        rows, w_in, w_qkv[0], w_out[0], w_up[0], w_down[0], norm_gains[0], final_gain[None],
        w_score[None],
    )
    scored = pl.pallas_call(
        functools.partial(slate_kernel, block=128),
        grid=(slates,),
        in_specs=[pl.BlockSpec(memory_space=pltpu.SMEM)]
        + [pl.BlockSpec(a.shape, lambda i: (0, 0)) for a in whole],
        out_specs=pl.BlockSpec((1, 1, length), lambda i: (i, 0, 0)),
        out_shape=jax.ShapeDtypeStruct((slates, 1, length), jnp.float32),
        scratch_shapes=[
            pltpu.VMEM((length, 3 * model), jnp.bfloat16),
            pltpu.VMEM((length, model), jnp.bfloat16),
            pltpu.VMEM(rows.shape, jnp.float32),
            pltpu.VMEM((2, length, rows.shape[1]), jnp.float32),
        ],
        compiler_params=pltpu.CompilerParams(vmem_limit_bytes=40 * 1024 * 1024),
        name="slates",
    )(place, *whole)
    return scored.reshape(slates, length)


def hops(move):
    return sum(min(part, 4 - part) for part in move[:3])


MOVES = sorted(
    ((x, y, z, c) for x in range(4) for y in range(4) for z in range(4) for c in range(2)),
    key=lambda move: -hops(move),
)[:-2] + [(0, 0, 0, 1)]


def number_kernel(owner_ref, row_ref, want_ref, place_ref, sums, flat, before, lower, *, shards, capacity):
    slates, _, slate = owner_ref.shape
    lower[...] = (
        lax.broadcasted_iota(jnp.int32, (slate, slate), 0)
        <= lax.broadcasted_iota(jnp.int32, (slate, slate), 1)
    ).astype(jnp.bfloat16)
    before[...] = jnp.zeros_like(before)
    sums[...] = jnp.zeros_like(sums)

    def number(s, carry):
        owner, row = owner_ref[s], row_ref[pl.ds(s, 1), :]
        own = lax.broadcasted_iota(jnp.int32, (shards, slate), 0) == owner
        onehot = own.astype(jnp.float32).astype(jnp.bfloat16)
        within = jnp.dot(onehot, lower[...], preferred_element_type=jnp.float32)
        count = jnp.sum(jnp.where(own, within + before[...], 0.0), axis=0, keepdims=True)
        slot = (count - 1.0).astype(jnp.int32)
        before[...] += within[:, slate - 1 :]
        place_ref[s] = owner * capacity + slot
        pick = lax.broadcasted_iota(jnp.int32, (capacity, slate), 0) == slot
        low, high = (row & 255).astype(jnp.float32), ((row >> 8) - 128).astype(jnp.float32)
        halves = jnp.concatenate([jnp.where(pick, low, 0.0), jnp.where(pick, high, 0.0)], axis=0)
        sums[...] += lax.dot_general(
            onehot, halves.astype(jnp.bfloat16), (((1,), (1,)), ((), ())),
            preferred_element_type=jnp.float32,
        )
        return carry

    lax.fori_loop(0, slates, number, 0)
    both = sums[...]
    flat[...] = (both + 256.0 * pltpu.roll(both, capacity, 1)).astype(jnp.int32) + 32768
    for shard in range(shards):
        want_ref[shard] = flat[shard : shard + 1, :]


def number_candidates(owner, row, shards, capacity):
    slates, _, slate = owner.shape
    lanes = 2 * capacity
    whole = pl.BlockSpec(memory_space=pltpu.VMEM)
    return pl.pallas_call(
        functools.partial(number_kernel, shards=shards, capacity=capacity),
        in_specs=[whole, whole],
        out_specs=(whole, whole),
        out_shape=(
            jax.ShapeDtypeStruct((shards, 1, lanes), jnp.int32),
            jax.ShapeDtypeStruct((slates, 1, slate), jnp.int32),
        ),
        scratch_shapes=[
            pltpu.VMEM((shards, lanes), jnp.float32),
            pltpu.VMEM((shards, lanes), jnp.int32),
            pltpu.VMEM((shards, 1), jnp.float32),
            pltpu.VMEM((slate, slate), jnp.bfloat16),
        ],
        compiler_params=pltpu.CompilerParams(vmem_limit_bytes=4 * 1024 * 1024),
        name="number",
    )(owner, row)


def exchange_kernel(
    want_ref, table_ref, out_ref, packed, table, block, sending, asked, numbers,
    chunk_sems, ask_send, ask_recv, row_send, row_recv, number_sem, *, shards, chunks, early, capacity,
):
    length = table_ref.shape[0] // chunks
    ring = packed.shape[0] // length
    gx, gy = lax.axis_index("gx"), lax.axis_index("gy")
    me = gx * 4 + gy
    x, y, core = gx // 8, (gx // 2) % 4, gx % 2
    xs = [((x + d) % 4) * 8 for d in range(4)]
    ys = [((y + d) % 4) * 2 for d in range(4)]
    zs = [(gy + d) % 4 for d in range(4)]
    cores = [core, 1 - core]

    def peer(move):
        to_gx, to_gy = xs[move[0]] + ys[move[1]] + cores[move[3]], zs[move[2]]
        return to_gx, to_gy, to_gx * 4 + to_gy

    def chunk_copy(chunk):
        source = table_ref.at[pl.ds(chunk * length, length)]
        target = packed.at[pl.ds((chunk % ring) * length, length)]
        return pltpu.make_async_copy(source, target, chunk_sems.at[chunk % ring])

    def load(chunk):
        chunk_copy(chunk).wait()

        def widen(part, carry):
            piece = packed[pl.ds((chunk % ring) * length + part * 128, 128)]
            table[pl.ds(chunk * length + part * 128, 128)] = piece.astype(jnp.float32)
            return carry

        lax.fori_loop(0, length // 128, widen, 0)
        if chunk + ring < chunks:
            chunk_copy(chunk + ring).start()

    for chunk in range(ring):
        chunk_copy(chunk).start()
    barrier = pltpu.get_barrier_semaphore()
    for move in MOVES:
        to_gx, to_gy, _ = peer(move)
        pl.semaphore_signal(barrier, inc=1, device_id=(to_gx, to_gy), device_id_type=MESH)
    for chunk in range(early):
        load(chunk)
    pl.semaphore_wait(barrier, shards - 1)
    for move in MOVES:
        to_gx, to_gy, shard = peer(move)
        pltpu.make_async_remote_copy(
            src_ref=want_ref.at[shard], dst_ref=asked.at[me], send_sem=ask_send, recv_sem=ask_recv,
            device_id=(to_gx, to_gy), device_id_type=MESH,
        ).start()
    asked[pl.ds(me, 1)] = want_ref[pl.ds(me, 1)]
    for chunk in range(early, chunks):
        load(chunk)
    others = pl.ds(0, shards - 1)
    pltpu.make_async_copy(asked.at[others], asked.at[others], ask_recv).wait()
    pltpu.make_async_copy(asked.at[others], asked.at[others], ask_send).wait()
    copy = pltpu.make_async_copy(asked, numbers, number_sem)
    copy.start()
    copy.wait()

    def collect(shard, target):
        for slot in range(capacity):
            block[pl.ds(slot, 1)] = table[pl.ds(numbers[shard, 0, slot], 1)]
        target[...] = block[...].astype(jnp.bfloat16)

    def receiver(step):
        a, b, c = step % 4, (step // 8) % 4, (step // 32) % 4
        to_gx = ((x + a) % 4) * 8 + ((y + a + b) % 4) * 2 + (core + (step // 4) % 2) % 2
        to_gy = (gy + a + c) % 4
        return to_gx, to_gy, to_gx * 4 + to_gy

    def send(step):
        to_gx, to_gy, shard = receiver(step)
        pltpu.make_async_remote_copy(
            src_ref=sending.at[shard], dst_ref=out_ref.at[me], send_sem=row_send, recv_sem=row_recv,
            device_id=(to_gx, to_gy), device_id_type=MESH,
        ).start()

    def give(step, carry):
        shard = receiver(step)[2]
        collect(shard, sending.at[shard])
        pl.when(step > 1)(lambda: send(step - 1))
        return carry

    lax.fori_loop(1, shards, give, 0)
    collect(me, out_ref.at[me])
    send(shards - 1)
    pltpu.make_async_copy(out_ref.at[others], out_ref.at[others], row_recv).wait()
    pltpu.make_async_copy(out_ref.at[others], out_ref.at[others], row_send).wait()


def exchange(want, item_table, capacity):
    shards, _, lanes = want.shape
    rows, width = item_table.shape
    chunks, ring, early = 12, 4, 4
    whole = pl.BlockSpec(memory_space=pltpu.VMEM)
    return pl.pallas_call(
        functools.partial(
            exchange_kernel, shards=shards, chunks=chunks, early=early, capacity=capacity
        ),
        in_specs=[whole, pl.BlockSpec(memory_space=pl.ANY)],
        out_specs=whole,
        out_shape=jax.ShapeDtypeStruct((shards, capacity, width), jnp.bfloat16),
        scratch_shapes=[
            pltpu.VMEM((rows // chunks * ring, width), jnp.bfloat16),
            pltpu.VMEM((rows, width), jnp.float32),
            pltpu.VMEM((capacity, width), jnp.float32),
            pltpu.VMEM((shards, capacity, width), jnp.bfloat16),
            pltpu.VMEM((shards, 1, lanes), jnp.int32),
            pltpu.SMEM((shards, 1, lanes), jnp.int32),
            pltpu.SemaphoreType.DMA((ring,)),
        ]
        + [pltpu.SemaphoreType.DMA] * 5,
        compiler_params=pltpu.CompilerParams(
            collective_id=0, has_side_effects=True, vmem_limit_bytes=52 * 1024 * 1024
        ),
        name="exchange",
    )(want, item_table)


def per_device(
    candidate_owner,
    candidate_row,
    item_table,
    w_in,
    w_qkv,
    w_out,
    w_up,
    w_down,
    norm_gains,
    final_gain,
    w_score,
):
    slates, length, unused = candidate_owner.shape
    width = item_table.shape[1]
    shards = lax.axis_size(("gx", "gy"))
    capacity = max(2, 2 * slates * length // shards)
    want, place = number_candidates(
        candidate_owner.reshape(slates, 1, length), candidate_row, shards, capacity
    )
    rows = exchange(want, item_table, capacity)
    rows = rows.reshape(shards * capacity, width)
    return score_slates(
        rows, place, w_in, w_qkv, w_out, w_up, w_down, norm_gains, final_gain, w_score
    )


def solution(mesh):
    return jax.shard_map(
        per_device,
        mesh=mesh,
        in_specs=(
            P(("gx", "gy"), None, None),
            P(("gx", "gy"), None),
            P(("gx", "gy"), None),
            P(),
            P(),
            P(),
            P(),
            P(),
            P(),
            P(),
            P(),
        ),
        out_specs=P(("gx", "gy"), None),
        check_vma=False,
    )
```

time: 152 us -> 108 us (0.71)
  local copies, waits for them, and re-layouts: 34.5 us -> 3.7 us
  Pallas kernels: 111 us -> 104 us
  other arithmetic: 5.18 us -> 0 us
    scatter x1 -> x0, local copies, waits for them, and re-layouts: 16.1 us -> none  [per_device(): jnp.zeros((shards * lanes,), jnp.int32).at[owner * lanes + slot]]
    gather x1 -> x0, local copies, waits for them, and re-layouts: 15 us -> none  [per_device(): emb = jnp.take(returned, position, axis=0).reshape(slates, length, width)]
    pallas_call x1, Pallas kernels: 59.3 us -> 46.5 us  [exchange(): pl.pallas_call(functools.partial(exchange_kernel, shards=shards, chunks=c...]
    pallas_call x1 -> x2, Pallas kernels: 51.8 us -> 57.7 us  [the longest x1 54 us: score_slates(): pl.pallas_call(functools.partial(slate_kernel, block=128), grid=(slates,)...]
    select_n x2 -> x0, other arithmetic: 2.19 us -> none  [per_device(): emb = jnp.take(returned, position, axis=0).reshape(slates, length, width)]
    unnamed x23, local copies, waits for them, and re-layouts: 2.14 us -> 3.69 us
where the time goes in v2:
time: 108 us
  Pallas kernels  104 us (96%)
  local copies, waits for them, and re-layouts  3.7 us (3%)
    pallas_call x1, Pallas kernels, score_slates(): pl.pallas_call(functools.partial(slate_kernel, block=128), grid=(slates,)...  54 us
    pallas_call x1, Pallas kernels, exchange(): pl.pallas_call(functools.partial(exchange_kernel, shards=shards, chunks=c...  46.5 us
    pallas_call x1, Pallas kernels, number_candidates(): pl.pallas_call(functools.partial(number_kernel, shards=shards, capacity=c...  3.7 us
    unnamed x23, local copies, waits for them, and re-layouts  3.69 us

profile of v2, /device:TPU:1, one launch (start us, length us, event | category | flops | bytes accessed | tf_op | source)
XLA Modules:
  0.0 108.1 jit_solution(14851929956610134117)
XLA Ops:
  0.0 0.0 copy-start.6
  0.0 0.7 copy-done.6
  0.7 0.0 copy-start.7
  0.7 0.7 copy-done.7
  1.4 3.7 %number.1 = (s32[128,1,128]{2,1,0:T(1,128)S(1)}, s32[8,1,512]{2,1,0:T(1,128)S(1)}) custom-call(s32[8,1,512]{2,1,0:T(1,128)S(1)} %bitcast.16, s32[8,512]{1,0:T(8,128)S(1)} %copy-done.7), custom_call_target="tpu_custom_call" | custom-call | tf_op jit(solution)/shard_map/number/pallas_call | solution.py:165
  5.1 0.0 copy-start.10
  5.2 0.0 copy-start.1
  5.2 0.0 copy-start.2
  5.2 0.0 copy-start.3
  5.2 0.0 copy-start.4
  5.2 0.0 copy-start.5
  5.2 0.0 copy-start.8
  5.2 0.0 copy-start.9
  5.2 46.5 %exchange.1 = bf16[128,64,128]{2,1,0:T(8,128)(2,1)} custom-call(s32[128,1,128]{2,1,0:T(1,128)S(1)} %get-tuple-element.8.want_ref, bf16[78336,128]{1,0:T(8,128)(2,1)} %table_ref.1), custom_call_target="tpu_custom_call" | custom-call | tf_op jit(solution)/shard_map/exchange/pallas_call | solution.py:280
  51.8 0.0 copy-done.10
  51.8 0.0 copy-done.1
  51.8 0.0 copy-done.2
  51.8 0.0 copy-done.3
  51.8 0.0 copy-done.4
  51.9 0.0 copy-done.5
  51.9 0.0 copy-done.8
  51.9 0.0 copy-done.9
  51.9 0.0 copy-start
  51.9 1.6 %copy-done = bf16[128,64,128]{2,1,0:T(8,128)(2,1)S(1)} copy-done((bf16[128,64,128]{2,1,0:T(8,128)(2,1)S(1)}, bf16[128,64,128]{2,1,0:T(8,128)(2,1)}, u32[]{:S(2)}) %copy-start) | copy-done | bytes 2097176
  53.5 54.0 %slates.1 = f32[8,1,512]{2,1,0:T(1,128)S(1)} custom-call(s32[8,1,512]{2,1,0:T(1,128)S(1)} %get-tuple-element.7.place_ref, bf16[8192,128]{1,0:T(8,128)(2,1)S(1)} %bitcast.11, bf16[128,512]{1,0:T(8,128)(2,1)S(1)} %copy-done.5, bf16[512,1536]{1,0:T(8,128)(2,1)S(1)} %bitcast.12, bf16[512,512]{1,0:T(8,128)(2,1)S(1)} %bitcast.15, bf16[512,1024]{1,0:T(8,128)(2,1)S(1)} %bitcast.13, ...), custom_call_target="tpu_custom_call" | custom-call | tf_op jit(solution)/shard_map/slates/pallas_call | solution.py:98
  107.5 0.6 copy.14
  (1 shorter events, 0.0 us)
Async XLA Ops:
  0.0 0.7 copy-start.6
  0.7 0.7 copy-start.7
  5.1 46.6 %copy-start.10 = (bf16[512]{0:T(512)(128)(2,1)S(1)}, bf16[512]{0:T(512)(128)(2,1)}, u32[]{:S(2)}) copy-start(bf16[512]{0:T(512)(128)(2,1)} %param.21) | copy-start | bytes 3076
  5.2 46.7 %copy-start.1 = (bf16[1,512,1536]{2,1,0:T(8,128)(2,1)S(1)}, bf16[1,512,1536]{2,1,0:T(8,128)(2,1)}, u32[]{:S(2)}) copy-start(bf16[1,512,1536]{2,1,0:T(8,128)(2,1)} %param.15) | copy-start | bytes 4718596
  5.2 46.7 %copy-start.2 = (bf16[1,512,1024]{2,1,0:T(8,128)(2,1)S(1)}, bf16[1,512,1024]{2,1,0:T(8,128)(2,1)}, u32[]{:S(2)}) copy-start(bf16[1,512,1024]{2,1,0:T(8,128)(2,1)} %param.17) | copy-start | bytes 3145732
  5.2 46.7 %copy-start.3 = (bf16[1,1024,512]{2,1,0:T(8,128)(2,1)S(1)}, bf16[1,1024,512]{2,1,0:T(8,128)(2,1)}, u32[]{:S(2)}) copy-start(bf16[1,1024,512]{2,1,0:T(8,128)(2,1)} %param.18) | copy-start | bytes 3145732
  5.2 46.7 %copy-start.4 = (bf16[1,512,512]{2,1,0:T(8,128)(2,1)S(1)}, bf16[1,512,512]{2,1,0:T(8,128)(2,1)}, u32[]{:S(2)}) copy-start(bf16[1,512,512]{2,1,0:T(8,128)(2,1)} %param.16) | copy-start | bytes 1572868
  5.2 46.6 %copy-start.5 = (bf16[128,512]{1,0:T(8,128)(2,1)S(1)}, bf16[128,512]{1,0:T(8,128)(2,1)}, u32[]{:S(2)}) copy-start(bf16[128,512]{1,0:T(8,128)(2,1)} %w_in_ref.1) | copy-start | bytes 393220
  5.2 46.6 %copy-start.8 = (f32[1,2,512]{2,1,0:T(2,128)S(1)}, f32[1,2,512]{2,1,0:T(2,128)}, u32[]{:S(2)}) copy-start(f32[1,2,512]{2,1,0:T(2,128)} %param.19) | copy-start | bytes 12292
  5.2 46.6 %copy-start.9 = (f32[512]{0:T(512)S(1)}, f32[512]{0:T(512)}, u32[]{:S(2)}) copy-start(f32[512]{0:T(512)} %param.20) | copy-start | bytes 6148
  51.9 1.6 %copy-start = (bf16[128,64,128]{2,1,0:T(8,128)(2,1)S(1)}, bf16[128,64,128]{2,1,0:T(8,128)(2,1)}, u32[]{:S(2)}) copy-start(bf16[128,64,128]{2,1,0:T(8,128)(2,1)} %exchange.1) | copy-start | bytes 6291460

commit v3 on v2

v3 whole, which is shorter than its diff:
```python
import functools

import jax
import jax.numpy as jnp
from jax import lax
from jax.experimental import pallas as pl
from jax.experimental.pallas import tpu as pltpu
from jax.sharding import PartitionSpec as P

MESH = pl.DeviceIdType.MESH
TOGETHER = 2


def layer_norm(values, gain):
    mean = jnp.mean(values, axis=-1, keepdims=True)
    centred = values - mean
    variance = jnp.mean(centred * centred, axis=-1, keepdims=True)
    return centred * lax.rsqrt(variance + 1e-05) * gain


def slate_kernel(
    place_ref, rows_ref, w_in_ref, w_qkv_ref, w_out_ref, w_up_ref, w_down_ref, gains_ref, final_ref,
    score_ref, out_ref, resid_ref, qkv_ref, mixed_ref, packed_ref, wide_ref, emb_ref, piece_sems, *, block,
):
    together, length, model = mixed_ref.shape
    slates = range(together)
    step = pl.program_id(0)
    now, later = step % 2, (step + 1) % 2
    following = jnp.minimum(step + 1, pl.num_programs(0) - 1) * together

    @pl.when(step == 0)
    def _():
        pieces = piece_sems.shape[0]
        count = rows_ref.shape[0] // pieces
        copies = [
            pltpu.make_async_copy(
                rows_ref.at[pl.ds(p * count, count)], packed_ref.at[pl.ds(p * count, count)], piece_sems.at[p]
            )
            for p in range(pieces)
        ]
        for copy in copies:
            copy.start()
        for p, copy in enumerate(copies):
            copy.wait()

            def widen(part, carry):
                piece = pl.ds(pl.multiple_of(p * count + part * 256, 256), 256)
                wide_ref[piece] = packed_ref[piece].astype(jnp.float32)
                return carry

            lax.fori_loop(0, count // 256, widen, 0)

        def fetch(part, carry):
            first = pl.multiple_of(part * 32, 32)
            for s in slates:
                for r in range(32):
                    row = wide_ref[pl.ds(place_ref[s, 0, first + r], 1)]
                    emb_ref[0, s, pl.ds(first + r, 1)] = row
            return carry

        lax.fori_loop(0, length // 32, fetch, 0)

    def matmul(values, weights_ref):
        return jnp.dot(values, weights_ref[...], preferred_element_type=jnp.float32)

    def add_resid(s, values):
        total = resid_ref[s] + values
        resid_ref[s] = total
        return total

    def beside(first, second, values):
        results, held = [], None
        for s in slates:
            passed = first(s, values[s])
            if s:
                results.append(second(s - 1, held))
            held = passed
        return results + [second(together - 1, held)]

    def project(s, normed):
        qkv_ref[s] = matmul(normed, w_qkv_ref).astype(jnp.bfloat16)

    def start(s):
        resid_ref[s] = matmul(emb_ref[now, s].astype(jnp.bfloat16), w_in_ref)
        return resid_ref[s]

    def normalise(row):
        gain = gains_ref[row : row + 1, :]
        return lambda s, values: layer_norm(values, gain).astype(jnp.bfloat16)

    beside(normalise(0), project, [start(s) for s in slates])

    low = lax.broadcasted_iota(jnp.int32, (1, 128), 1) < 64
    scales = (
        jnp.where(low, 0.125, 0.0).astype(jnp.bfloat16),
        jnp.where(low, 0.0, 0.125).astype(jnp.bfloat16),
    )
    ones = jnp.ones((length, 128), jnp.bfloat16)
    pieces = [
        (s, column, row)
        for column in range(0, model, 128)
        for s in slates
        for row in range(0, length, block)
    ]
    share = together * length // len(pieces)
    for part, (s, column, row) in enumerate(pieces):
        for r in range(part * share, (part + 1) * share):
            ahead, r = divmod(r, length)
            fetched = wide_ref[pl.ds(place_ref[following + ahead, 0, r], 1)]
            emb_ref[later, ahead, pl.ds(r, 1)] = fetched
        query = qkv_ref[s, row : row + block, column : column + 128]
        keys = qkv_ref[s, :, model + column : model + column + 128]
        values = qkv_ref[s, :, 2 * model + column : 2 * model + column + 128]
        values = jnp.concatenate([values, ones], axis=1)
        heads = []
        for scale in scales:
            scores = lax.dot_general(
                query * scale, keys, (((1,), (1,)), ((), ())), preferred_element_type=jnp.float32
            )
            top = jnp.max(scores, axis=-1, keepdims=True)
            weights = jnp.exp(scores - top).astype(jnp.bfloat16)
            heads.append(jnp.dot(weights, values, preferred_element_type=jnp.float32))
        sums = jnp.where(low, heads[0][:, 128:], heads[1][:, 128:])
        mixed = jnp.where(low, heads[0][:, :128], heads[1][:, :128]) / sums
        mixed_ref[s, row : row + block, column : column + 128] = mixed.astype(jnp.bfloat16)

    resid = [add_resid(s, matmul(mixed_ref[s], w_out_ref)) for s in slates]
    raised = beside(normalise(1), lambda s, normed: matmul(normed, w_up_ref), resid)
    lowered = beside(
        lambda s, values: jax.nn.gelu(values).astype(jnp.bfloat16),
        lambda s, inner: matmul(inner, w_down_ref),
        raised,
    )
    for s in slates:
        final = layer_norm(resid_ref[s] + lowered[s], final_ref[...])
        logits = jnp.sum(final * score_ref[...].astype(jnp.float32), axis=-1).reshape(1, length)
        shifted = logits - jnp.max(logits, axis=-1, keepdims=True)
        total = jnp.sum(jnp.exp(shifted), axis=-1, keepdims=True)
        out_ref[s] = shifted - jnp.log(total)


def score_slates(rows, place, w_in, w_qkv, w_out, w_up, w_down, norm_gains, final_gain, w_score):
    slates, _, length = place.shape
    model = w_in.shape[1]
    together = TOGETHER
    whole = (
        rows, w_in, w_qkv[0], w_out[0], w_up[0], w_down[0], norm_gains[0], final_gain[None],
        w_score[None],
    )
    scored = pl.pallas_call(
        functools.partial(slate_kernel, block=128),
        grid=(slates // together,),
        in_specs=[pl.BlockSpec(memory_space=pltpu.SMEM), pl.BlockSpec(memory_space=pl.ANY)]
        + [pl.BlockSpec(a.shape, lambda i: (0, 0)) for a in whole[1:]],
        out_specs=pl.BlockSpec((together, 1, length), lambda i: (i, 0, 0)),
        out_shape=jax.ShapeDtypeStruct((slates, 1, length), jnp.float32),
        scratch_shapes=[
            pltpu.VMEM((together, length, model), jnp.float32),
            pltpu.VMEM((together, length, 3 * model), jnp.bfloat16),
            pltpu.VMEM((together, length, model), jnp.bfloat16),
            pltpu.VMEM(rows.shape, jnp.bfloat16),
            pltpu.VMEM(rows.shape, jnp.float32),
            pltpu.VMEM((2, together, length, rows.shape[1]), jnp.float32),
            pltpu.SemaphoreType.DMA((8,)),
        ],
        compiler_params=pltpu.CompilerParams(vmem_limit_bytes=48 * 1024 * 1024),
        name="slates",
    )(place, *whole)
    return scored.reshape(slates, length)


def hops(move):
    return sum(min(part, 4 - part) for part in move[:3])


def move_of(group, member):
    a = member % 4
    return a, (a + group[0]) % 4, (a + group[1]) % 4, member // 4


MEMBERS = 8
GROUPS = sorted(
    ((b, c) for b in range(4) for c in range(4)),
    key=lambda group: max(hops(move_of(group, member)) for member in range(MEMBERS)),
)
GROUPS = GROUPS[:6] + GROUPS[:5:-1]
MOVES = [(group, member) for group in GROUPS for member in range(MEMBERS)]
MOVES.remove(((0, 0), 0))


def back(group, member):
    return GROUPS.index((-group[0] % 4, -group[1] % 4)), -member % 4 + member // 4 * 4


def number_kernel(owner_ref, row_ref, want_ref, place_ref, flat, lower, *, shards, capacity):
    slates, _, slate = owner_ref.shape
    lower[...] = (
        lax.broadcasted_iota(jnp.int32, (slate, slate), 0)
        <= lax.broadcasted_iota(jnp.int32, (slate, slate), 1)
    ).astype(jnp.bfloat16)
    seen = jnp.zeros((shards, 1), jnp.float32)
    both = jnp.zeros((shards, 2 * capacity), jnp.float32)
    for s in range(slates):
        owner, row = owner_ref[s], row_ref[s : s + 1, :]
        own = lax.broadcasted_iota(jnp.int32, (shards, slate), 0) == owner
        onehot = own.astype(jnp.float32).astype(jnp.bfloat16)
        within = jnp.dot(onehot, lower[...], preferred_element_type=jnp.float32)
        count = jnp.sum(jnp.where(own, within + seen, 0.0), axis=0, keepdims=True)
        slot = (count - 1.0).astype(jnp.int32)
        seen = seen + within[:, slate - 1 :]
        place_ref[s] = owner * capacity + slot
        pick = lax.broadcasted_iota(jnp.int32, (capacity, slate), 0) == slot
        low, high = (row & 255).astype(jnp.float32), ((row >> 8) - 128).astype(jnp.float32)
        halves = jnp.concatenate([jnp.where(pick, low, 0.0), jnp.where(pick, high, 0.0)], axis=0)
        both = both + lax.dot_general(
            onehot, halves.astype(jnp.bfloat16), (((1,), (1,)), ((), ())),
            preferred_element_type=jnp.float32,
        )
    flat[...] = (both + 256.0 * pltpu.roll(both, capacity, 1)).astype(jnp.int32) + 32768
    for shard in range(shards):
        want_ref[shard] = flat[shard : shard + 1, :]


def number_candidates(owner, row, shards, capacity):
    slates, _, slate = owner.shape
    lanes = 2 * capacity
    whole = pl.BlockSpec(memory_space=pltpu.VMEM)
    return pl.pallas_call(
        functools.partial(number_kernel, shards=shards, capacity=capacity),
        in_specs=[whole, whole],
        out_specs=(whole, whole),
        out_shape=(
            jax.ShapeDtypeStruct((shards, 1, lanes), jnp.int32),
            jax.ShapeDtypeStruct((slates, 1, slate), jnp.int32),
        ),
        scratch_shapes=[
            pltpu.VMEM((shards, lanes), jnp.int32),
            pltpu.VMEM((slate, slate), jnp.bfloat16),
        ],
        compiler_params=pltpu.CompilerParams(vmem_limit_bytes=8 * 1024 * 1024),
        name="number",
    )(owner, row)


def exchange_kernel(
    want_ref, table_ref, out_ref, packed, table, block, sending, asked, numbers,
    chunk_sems, ask_send, ask_recv, row_send, row_recv, number_sems, own_sem,
    *, shards, chunks, early, capacity,
):
    length = table_ref.shape[0] // chunks
    ring = packed.shape[0] // length
    gx, gy = lax.axis_index("gx"), lax.axis_index("gy")
    me = gx * 4 + gy
    x, y, core = gx // 8, (gx // 2) % 4, gx % 2
    xs = [((x + d) % 4) * 8 for d in range(4)]
    ys = [((y + d) % 4) * 2 for d in range(4)]
    zs = [(gy + d) % 4 for d in range(4)]
    cores = [core, 1 - core]

    def peer(move):
        to_gx, to_gy = xs[move[0]] + ys[move[1]] + cores[move[3]], zs[move[2]]
        return to_gx, to_gy, to_gx * 4 + to_gy

    def chunk_copy(chunk):
        source = table_ref.at[pl.ds(chunk * length, length)]
        target = packed.at[pl.ds((chunk % ring) * length, length)]
        return pltpu.make_async_copy(source, target, chunk_sems.at[chunk % ring])

    def load(chunk):
        chunk_copy(chunk).wait()

        def widen(part, carry):
            piece = packed[pl.ds((chunk % ring) * length + part * 128, 128)]
            table[pl.ds(chunk * length + part * 128, 128)] = piece.astype(jnp.float32)
            return carry

        lax.fori_loop(0, length // 128, widen, 0)
        if chunk + ring < chunks:
            chunk_copy(chunk + ring).start()

    for chunk in range(ring):
        chunk_copy(chunk).start()
    barrier = pltpu.get_barrier_semaphore()
    for group, member in reversed(MOVES):
        to_gx, to_gy, _ = peer(move_of(group, member))
        pl.semaphore_signal(barrier, inc=1, device_id=(to_gx, to_gy), device_id_type=MESH)
    for chunk in range(early):
        load(chunk)
    pl.semaphore_wait(barrier, shards - 1)
    for group, member in sorted(MOVES, key=lambda move: back(*move)):
        to_gx, to_gy, shard = peer(move_of(group, member))
        there, place = back(group, member)
        pltpu.make_async_remote_copy(
            src_ref=want_ref.at[shard], dst_ref=asked.at[there * MEMBERS + place],
            send_sem=ask_send, recv_sem=ask_recv.at[there],
            device_id=(to_gx, to_gy), device_id_type=MESH,
        ).start()
    home = GROUPS.index((0, 0))
    asked[pl.ds(home * MEMBERS, 1)] = want_ref[pl.ds(me, 1)]
    for chunk in range(early, chunks):
        load(chunk)

    def number_copy(number):
        members = pl.ds(number * MEMBERS, MEMBERS)
        return pltpu.make_async_copy(asked.at[members], numbers.at[members], number_sems.at[number])

    def hear(number):
        heard = pl.ds(number * MEMBERS, MEMBERS)
        if number == home:
            heard = pl.ds(number * MEMBERS + 1, MEMBERS - 1)
        pltpu.make_async_copy(asked.at[heard], asked.at[heard], ask_recv.at[number]).wait()
        number_copy(number).start()

    def collect(place, shard):
        for slot in range(capacity):
            block[pl.ds(slot, 1)] = table[pl.ds(numbers[place, 0, slot], 1)]
        sending[shard] = block[...].astype(jnp.bfloat16)

    def receiver(group, member):
        a = member % 4
        to_gx = ((x + a) % 4) * 8 + ((y + a + group[0]) % 4) * 2 + (core + member // 4) % 2
        to_gy = (gy + a + group[1]) % 4
        return to_gx, to_gy, to_gx * 4 + to_gy

    def send(group, member):
        to_gx, to_gy, shard = receiver(group, member)
        pltpu.make_async_remote_copy(
            src_ref=sending.at[shard], dst_ref=out_ref.at[me], send_sem=row_send, recv_sem=row_recv,
            device_id=(to_gx, to_gy), device_id_type=MESH,
        ).start()

    hear(0)
    for number, group in enumerate(GROUPS):
        if number + 1 < len(GROUPS):
            hear(number + 1)
        number_copy(number).wait()
        if number:
            send(GROUPS[number - 1], MEMBERS - 1)
        first = 1 if number == home else 0

        def give(member, carry):
            collect(number * MEMBERS + member, receiver(group, member)[2])
            pl.when(member > first)(lambda: send(group, member - 1))
            return carry

        lax.fori_loop(first, MEMBERS, give, 0)
    collect(home * MEMBERS, me)
    send(GROUPS[-1], MEMBERS - 1)
    others = pl.ds(0, shards - 1)
    pltpu.make_async_copy(asked.at[others], asked.at[others], ask_send).wait()
    own = pltpu.make_async_copy(sending.at[me], out_ref.at[me], own_sem)
    own.start()
    own.wait()
    pltpu.make_async_copy(sending.at[others], sending.at[others], row_recv).wait()
    pltpu.make_async_copy(sending.at[others], sending.at[others], row_send).wait()


def exchange(want, item_table, capacity):
    shards, _, lanes = want.shape
    rows, width = item_table.shape
    chunks, ring, early = 12, 4, 6
    whole, anywhere = pl.BlockSpec(memory_space=pltpu.VMEM), pl.BlockSpec(memory_space=pl.ANY)
    return pl.pallas_call(
        functools.partial(
            exchange_kernel, shards=shards, chunks=chunks, early=early, capacity=capacity
        ),
        in_specs=[whole, anywhere],
        out_specs=anywhere,
        out_shape=jax.ShapeDtypeStruct((shards, capacity, width), jnp.bfloat16),
        scratch_shapes=[
            pltpu.VMEM((rows // chunks * ring, width), jnp.bfloat16),
            pltpu.VMEM((rows, width), jnp.float32),
            pltpu.VMEM((capacity, width), jnp.float32),
            pltpu.VMEM((shards, capacity, width), jnp.bfloat16),
            pltpu.VMEM((shards, 1, lanes), jnp.int32),
            pltpu.SMEM((shards, 1, lanes), jnp.int32),
            pltpu.SemaphoreType.DMA((ring,)),
            pltpu.SemaphoreType.DMA,
            pltpu.SemaphoreType.DMA((len(GROUPS),)),
            pltpu.SemaphoreType.DMA,
            pltpu.SemaphoreType.DMA,
            pltpu.SemaphoreType.DMA((len(GROUPS),)),
            pltpu.SemaphoreType.DMA,
        ],
        compiler_params=pltpu.CompilerParams(
            collective_id=0, has_side_effects=True, vmem_limit_bytes=52 * 1024 * 1024
        ),
        name="exchange",
    )(want, item_table)


def per_device(
    candidate_owner,
    candidate_row,
    item_table,
    w_in,
    w_qkv,
    w_out,
    w_up,
    w_down,
    norm_gains,
    final_gain,
    w_score,
):
    slates, length, unused = candidate_owner.shape
    width = item_table.shape[1]
    shards = lax.axis_size(("gx", "gy"))
    capacity = max(2, 2 * slates * length // shards)
    want, place = number_candidates(
        candidate_owner.reshape(slates, 1, length), candidate_row, shards, capacity
    )
    rows = exchange(want, item_table, capacity)
    rows = rows.reshape(shards * capacity, width)
    return score_slates(
        rows, place, w_in, w_qkv, w_out, w_up, w_down, norm_gains, final_gain, w_score
    )


def solution(mesh):
    return jax.shard_map(
        per_device,
        mesh=mesh,
        in_specs=(
            P(("gx", "gy"), None, None),
            P(("gx", "gy"), None),
            P(("gx", "gy"), None),
            P(),
            P(),
            P(),
            P(),
            P(),
            P(),
            P(),
            P(),
        ),
        out_specs=P(("gx", "gy"), None),
        check_vma=False,
    )
```

time: 108 us -> 97.5 us (0.903)
  Pallas kernels: 104 us -> 94.9 us
  local copies, waits for them, and re-layouts: 3.7 us -> 2.1 us
    pallas_call x1, Pallas kernels: 54 us -> 49.2 us  [score_slates(): pl.pallas_call(functools.partial(slate_kernel, block=128), grid=(slates /...]
    pallas_call x1, Pallas kernels: 46.5 us -> 43.9 us  [exchange(): pl.pallas_call(functools.partial(exchange_kernel, shards=shards, chunks=c...]
    pallas_call x1, Pallas kernels: 3.7 us -> 1.83 us  [number_candidates(): pl.pallas_call(functools.partial(number_kernel, shards=shards, capacity=c...]
    unnamed x23 -> x21, local copies, waits for them, and re-layouts: 3.69 us -> 2.09 us
where the time goes in v3:
time: 97.5 us; the launch traced here: 97.2 us
  Pallas kernels  94.9 us (97%)
  local copies, waits for them, and re-layouts  2.1 us (2%)
    pallas_call x1, Pallas kernels, score_slates(): pl.pallas_call(functools.partial(slate_kernel, block=128), grid=(slates /...  49.2 us
    pallas_call x1, Pallas kernels, exchange(): pl.pallas_call(functools.partial(exchange_kernel, shards=shards, chunks=c...  43.9 us
    unnamed x21, local copies, waits for them, and re-layouts  2.09 us

profile of v3, /device:TPU:1, one launch (start us, length us, event | category | flops | bytes accessed | tf_op | source)
XLA Modules:
  0.0 97.2 jit_solution(12578126128974595358)
XLA Ops:
  0.0 0.0 copy-start.5
  0.0 0.7 copy-done.5
  0.7 0.0 copy-start.6
  0.7 0.7 copy-done.6
  1.4 1.8 %number.1 = (s32[128,1,128]{2,1,0:T(1,128)S(1)}, s32[8,1,512]{2,1,0:T(1,128)S(1)}) custom-call(s32[8,1,512]{2,1,0:T(1,128)S(1)} %bitcast.15, s32[8,512]{1,0:T(8,128)S(1)} %copy-done.6), custom_call_target="tpu_custom_call" | custom-call | tf_op jit(solution)/shard_map/number/pallas_call | solution.py:228
  3.3 0.0 copy-start.9
  3.3 0.0 copy-start
  3.3 0.0 copy-start.1
  3.3 0.0 copy-start.2
  3.3 0.0 copy-start.3
  3.3 0.0 copy-start.4
  3.3 0.0 copy-start.7
  3.4 0.0 copy-start.8
  3.4 43.9 %exchange.1 = bf16[128,64,128]{2,1,0:T(8,128)(2,1)} custom-call(s32[128,1,128]{2,1,0:T(1,128)S(1)} %get-tuple-element.8.want_ref, bf16[78336,128]{1,0:T(8,128)(2,1)} %table_ref.1), custom_call_target="tpu_custom_call" | custom-call | tf_op jit(solution)/shard_map/exchange/pallas_call | solution.py:363
  47.3 0.0 copy-done.9
  47.3 0.0 copy-done
  47.3 0.0 copy-done.1
  47.3 0.0 copy-done.2
  47.3 0.0 copy-done.3
  47.3 0.0 copy-done.4
  47.3 0.0 copy-done.7
  47.3 0.0 copy-done.8
  47.4 49.2 %slates.1 = f32[8,1,512]{2,1,0:T(1,128)S(1)} custom-call(s32[8,1,512]{2,1,0:T(1,128)S(1)} %get-tuple-element.7.place_ref, bf16[8192,128]{1,0:T(8,128)(2,1)} %bitcast.18, bf16[128,512]{1,0:T(8,128)(2,1)S(1)} %copy-done.4, bf16[512,1536]{1,0:T(8,128)(2,1)S(1)} %bitcast.11, bf16[512,512]{1,0:T(8,128)(2,1)S(1)} %bitcast.14, bf16[512,1024]{1,0:T(8,128)(2,1)S(1)} %bitcast.12, ...), custom_call_target="tpu_custom_call" | custom-call | tf_op jit(solution)/shard_map/slates/pallas_call | solution.py:150
  96.6 0.6 copy.14
  (1 shorter events, 0.0 us)
Async XLA Ops:
  0.0 0.7 copy-start.5
  0.7 0.7 copy-start.6
  3.3 44.0 %copy-start.9 = (bf16[512]{0:T(512)(128)(2,1)S(1)}, bf16[512]{0:T(512)(128)(2,1)}, u32[]{:S(2)}) copy-start(bf16[512]{0:T(512)(128)(2,1)} %param.21) | copy-start | bytes 3076
  3.3 44.0 %copy-start = (bf16[1,512,1536]{2,1,0:T(8,128)(2,1)S(1)}, bf16[1,512,1536]{2,1,0:T(8,128)(2,1)}, u32[]{:S(2)}) copy-start(bf16[1,512,1536]{2,1,0:T(8,128)(2,1)} %param.15) | copy-start | bytes 4718596
  3.3 44.0 %copy-start.1 = (bf16[1,512,1024]{2,1,0:T(8,128)(2,1)S(1)}, bf16[1,512,1024]{2,1,0:T(8,128)(2,1)}, u32[]{:S(2)}) copy-start(bf16[1,512,1024]{2,1,0:T(8,128)(2,1)} %param.17) | copy-start | bytes 3145732
  3.3 44.0 %copy-start.2 = (bf16[1,1024,512]{2,1,0:T(8,128)(2,1)S(1)}, bf16[1,1024,512]{2,1,0:T(8,128)(2,1)}, u32[]{:S(2)}) copy-start(bf16[1,1024,512]{2,1,0:T(8,128)(2,1)} %param.18) | copy-start | bytes 3145732
  3.3 44.0 %copy-start.3 = (bf16[1,512,512]{2,1,0:T(8,128)(2,1)S(1)}, bf16[1,512,512]{2,1,0:T(8,128)(2,1)}, u32[]{:S(2)}) copy-start(bf16[1,512,512]{2,1,0:T(8,128)(2,1)} %param.16) | copy-start | bytes 1572868
  3.3 44.0 %copy-start.4 = (bf16[128,512]{1,0:T(8,128)(2,1)S(1)}, bf16[128,512]{1,0:T(8,128)(2,1)}, u32[]{:S(2)}) copy-start(bf16[128,512]{1,0:T(8,128)(2,1)} %w_in_ref.1) | copy-start | bytes 393220
  3.3 44.0 %copy-start.7 = (f32[1,2,512]{2,1,0:T(2,128)S(1)}, f32[1,2,512]{2,1,0:T(2,128)}, u32[]{:S(2)}) copy-start(f32[1,2,512]{2,1,0:T(2,128)} %param.19) | copy-start | bytes 12292
  3.4 44.0 %copy-start.8 = (f32[512]{0:T(512)S(1)}, f32[512]{0:T(512)}, u32[]{:S(2)}) copy-start(f32[512]{0:T(512)} %param.20) | copy-start | bytes 6148

commit v4 on v3

--- a/solution.py
+++ b/solution.py
@@ -8,7 +8,7 @@
 from jax.sharding import PartitionSpec as P
 
 MESH = pl.DeviceIdType.MESH
-TOGETHER = 2
+TOGETHER = 4
 
 
 def layer_norm(values, gain):
@@ -52,10 +52,9 @@
 
         def fetch(part, carry):
             first = pl.multiple_of(part * 32, 32)
-            for s in slates:
-                for r in range(32):
-                    row = wide_ref[pl.ds(place_ref[s, 0, first + r], 1)]
-                    emb_ref[0, s, pl.ds(first + r, 1)] = row
+            for r in range(32):
+                row = wide_ref[pl.ds(place_ref[0, 0, first + r], 1)]
+                emb_ref[0, 0, pl.ds(first + r, 1)] = row
             return carry
 
         lax.fori_loop(0, length // 32, fetch, 0)
@@ -81,6 +80,10 @@
         qkv_ref[s] = matmul(normed, w_qkv_ref).astype(jnp.bfloat16)
 
     def start(s):
+        if s:
+            for r in range(length):
+                row = wide_ref[pl.ds(place_ref[step * together + s, 0, r], 1)]
+                emb_ref[now, s, pl.ds(r, 1)] = row
         resid_ref[s] = matmul(emb_ref[now, s].astype(jnp.bfloat16), w_in_ref)
         return resid_ref[s]
 
@@ -88,7 +91,8 @@
         gain = gains_ref[row : row + 1, :]
         return lambda s, values: layer_norm(values, gain).astype(jnp.bfloat16)
 
-    beside(normalise(0), project, [start(s) for s in slates])
+    first_norm = normalise(0)
+    beside(lambda s, _: first_norm(s, start(s)), project, [None] * together)
 
     low = lax.broadcasted_iota(jnp.int32, (1, 128), 1) < 64
     scales = (
@@ -102,7 +106,7 @@
         for s in slates
         for row in range(0, length, block)
     ]
-    share = together * length // len(pieces)
+    share = length // len(pieces)
     for part, (s, column, row) in enumerate(pieces):
         for r in range(part * share, (part + 1) * share):
             ahead, r = divmod(r, length)

time: 97.5 us -> 95.3 us (0.977)
  Pallas kernels: 94.9 us -> 92.7 us
    pallas_call x1, Pallas kernels: 49.2 us -> 47 us  [score_slates(): pl.pallas_call(functools.partial(slate_kernel, block=128), grid=(slates /...]
where the time goes in v4:
time: 95.3 us; the launch traced here: 95 us
  Pallas kernels  92.7 us (97%)
  local copies, waits for them, and re-layouts  2.1 us (2%)
    pallas_call x1, Pallas kernels, score_slates(): pl.pallas_call(functools.partial(slate_kernel, block=128), grid=(slates /...  47 us
    pallas_call x1, Pallas kernels, exchange(): pl.pallas_call(functools.partial(exchange_kernel, shards=shards, chunks=c...  43.9 us
    unnamed x21, local copies, waits for them, and re-layouts  2.09 us

profile of v4, /device:TPU:1, one launch (start us, length us, event | category | flops | bytes accessed | tf_op | source)
XLA Modules:
  0.0 95.0 jit_solution(6292622642234947750)
XLA Ops:
  0.0 0.0 copy-start.5
  0.0 0.7 copy-done.5
  0.7 0.0 copy-start.6
  0.7 0.7 copy-done.6
  1.4 1.8 %number.1 = (s32[128,1,128]{2,1,0:T(1,128)S(1)}, s32[8,1,512]{2,1,0:T(1,128)S(1)}) custom-call(s32[8,1,512]{2,1,0:T(1,128)S(1)} %bitcast.15, s32[8,512]{1,0:T(8,128)S(1)} %copy-done.6), custom_call_target="tpu_custom_call" | custom-call | tf_op jit(solution)/shard_map/number/pallas_call | solution.py:232
  3.3 0.0 copy-start.9
  3.3 0.0 copy-start
  3.3 0.0 copy-start.1
  3.3 0.0 copy-start.2
  3.3 0.0 copy-start.3
  3.3 0.0 copy-start.4
  3.3 0.0 copy-start.7
  3.4 0.0 copy-start.8
  3.4 43.9 %exchange.1 = bf16[128,64,128]{2,1,0:T(8,128)(2,1)} custom-call(s32[128,1,128]{2,1,0:T(1,128)S(1)} %get-tuple-element.8.want_ref, bf16[78336,128]{1,0:T(8,128)(2,1)} %table_ref.1), custom_call_target="tpu_custom_call" | custom-call | tf_op jit(solution)/shard_map/exchange/pallas_call | solution.py:367
  47.3 0.0 copy-done.9
  47.3 0.0 copy-done
  47.3 0.0 copy-done.1
  47.3 0.0 copy-done.2
  47.3 0.0 copy-done.3
  47.3 0.0 copy-done.4
  47.3 0.0 copy-done.7
  47.4 0.0 copy-done.8
  47.4 47.0 %slates.1 = f32[8,1,512]{2,1,0:T(1,128)S(1)} custom-call(s32[8,1,512]{2,1,0:T(1,128)S(1)} %get-tuple-element.7.place_ref, bf16[8192,128]{1,0:T(8,128)(2,1)} %bitcast.18, bf16[128,512]{1,0:T(8,128)(2,1)S(1)} %copy-done.4, bf16[512,1536]{1,0:T(8,128)(2,1)S(1)} %bitcast.11, bf16[512,512]{1,0:T(8,128)(2,1)S(1)} %bitcast.14, bf16[512,1024]{1,0:T(8,128)(2,1)S(1)} %bitcast.12, ...), custom_call_target="tpu_custom_call" | custom-call | tf_op jit(solution)/shard_map/slates/pallas_call | solution.py:154
  94.4 0.6 copy.14
  (1 shorter events, 0.0 us)
Async XLA Ops:
  0.0 0.7 copy-start.5
  0.7 0.7 copy-start.6
  3.3 44.0 %copy-start.9 = (bf16[512]{0:T(512)(128)(2,1)S(1)}, bf16[512]{0:T(512)(128)(2,1)}, u32[]{:S(2)}) copy-start(bf16[512]{0:T(512)(128)(2,1)} %param.21) | copy-start | bytes 3076
  3.3 44.0 %copy-start = (bf16[1,512,1536]{2,1,0:T(8,128)(2,1)S(1)}, bf16[1,512,1536]{2,1,0:T(8,128)(2,1)}, u32[]{:S(2)}) copy-start(bf16[1,512,1536]{2,1,0:T(8,128)(2,1)} %param.15) | copy-start | bytes 4718596
  3.3 44.0 %copy-start.1 = (bf16[1,512,1024]{2,1,0:T(8,128)(2,1)S(1)}, bf16[1,512,1024]{2,1,0:T(8,128)(2,1)}, u32[]{:S(2)}) copy-start(bf16[1,512,1024]{2,1,0:T(8,128)(2,1)} %param.17) | copy-start | bytes 3145732
  3.3 44.0 %copy-start.2 = (bf16[1,1024,512]{2,1,0:T(8,128)(2,1)S(1)}, bf16[1,1024,512]{2,1,0:T(8,128)(2,1)}, u32[]{:S(2)}) copy-start(bf16[1,1024,512]{2,1,0:T(8,128)(2,1)} %param.18) | copy-start | bytes 3145732
  3.3 44.0 %copy-start.3 = (bf16[1,512,512]{2,1,0:T(8,128)(2,1)S(1)}, bf16[1,512,512]{2,1,0:T(8,128)(2,1)}, u32[]{:S(2)}) copy-start(bf16[1,512,512]{2,1,0:T(8,128)(2,1)} %param.16) | copy-start | bytes 1572868
  3.3 44.0 %copy-start.4 = (bf16[128,512]{1,0:T(8,128)(2,1)S(1)}, bf16[128,512]{1,0:T(8,128)(2,1)}, u32[]{:S(2)}) copy-start(bf16[128,512]{1,0:T(8,128)(2,1)} %w_in_ref.1) | copy-start | bytes 393220
  3.3 44.0 %copy-start.7 = (f32[1,2,512]{2,1,0:T(2,128)S(1)}, f32[1,2,512]{2,1,0:T(2,128)}, u32[]{:S(2)}) copy-start(f32[1,2,512]{2,1,0:T(2,128)} %param.19) | copy-start | bytes 12292
  3.4 44.0 %copy-start.8 = (f32[512]{0:T(512)S(1)}, f32[512]{0:T(512)}, u32[]{:S(2)}) copy-start(f32[512]{0:T(512)} %param.20) | copy-start | bytes 6148
